TPU v7x, 256 devices: a whole 4x4x8 slice. The times are simulated.
256 devices in a mesh: gx: 8 (over z_lo, core), gy: 4 (over y), gz: 8 (over z_hi, x).
Axes of the slice: x: 4, y: 4, z: 8 (z_hi: 2, z_lo: 4; z = z_hi * 4 + z_lo), core: 2. Of those that a mesh axis runs over, the one named last changes fastest.
Arguments:
- raw_weight: float32 [128, 27, 128], P(('gx', 'gy')), may hold values from -6 to 6
- inputs: bfloat16 [64, 64, 128, 128], P('gx', 'gy', 'gz'), may hold values from -6 to 6
- cotangent: bfloat16 [64, 64, 128, 128], P('gx', 'gy', 'gz'), may hold values from -0.099609375 to 0.099609375
Outputs:
- input_grad: bfloat16 [64, 64, 128, 128], P('gx', 'gy', 'gz')
- weight_grad: float32 [128, 27, 128], P(('gx', 'gy'))
All inputs are finite; a program needn't handle non-finite values.
Results may differ from a plain program's by a relative error of at most 0.0049.
Values may be sent and summed in bfloat16 or wider, within the bound.
A program may use at most 64 MiB of HBM per device.

v0:
```python
import jax
import jax.numpy as jnp
from jax import lax
from jax.sharding import PartitionSpec as P

var_eps = 1e-05
norm_eps = 1e-06
clip_norm = 600.0


def with_halo(cells, sides, width):
    for axis, dim in sides:
        count = lax.axis_size(axis)
        ends = count - 1
        head = lax.slice_in_dim(cells, 0, width, axis=dim)
        tail = lax.slice_in_dim(cells, cells.shape[dim] - width, cells.shape[dim], axis=dim)
        cells = jnp.concatenate(
            [
                lax.ppermute(tail, axis, [(i, (i + 1) % count) for i in range(ends)]),
                cells,
                lax.ppermute(head, axis, [((i + 1) % count, i) for i in range(ends)]),
            ],
            axis=dim,
        )
    return cells


def in_blocks(array, dim, peers):
    lengths = array.shape
    parts = array.reshape(*lengths[:dim], peers, lengths[dim] // peers, *lengths[dim + 1 :])
    return jnp.moveaxis(parts, dim, 0)


def sent_and_summed(array, axis, dim):
    peers = lax.axis_size(axis)
    parts = lax.all_to_all(in_blocks(array, dim, peers), axis, 0, 0, tiled=True)
    return jnp.sum(parts.astype(jnp.float32), axis=0)


def sent_to_all(array, axis):
    peers = lax.axis_size(axis)
    return lax.all_to_all(
        jnp.broadcast_to(array[None], (peers, *array.shape)), axis, 0, 0, tiled=True
    )


def of_everyone(array, axis):
    return sent_to_all(array, axis).sum(axis=0)


def together(arrays, axis):
    ends = [0]
    for a in arrays:
        ends.append(ends[-1] + a.size)
    so_far = of_everyone(jnp.concatenate([a.ravel() for a in arrays]), axis)
    return tuple((so_far[b:e].reshape(a.shape) for a, b, e in zip(arrays, ends, ends[1:])))


def tap_view(padded, tap_a, tap_b, tap_c, extent):
    view = padded[
        2 - tap_a : 2 - tap_a + extent[0],
        2 - tap_b : 2 - tap_b + extent[1],
        2 - tap_c : 2 - tap_c + extent[2],
        :,
    ]
    return view.reshape(-1, view.shape[-1])


def input_rows(padded, extent, block_rows):
    row_count = block_rows.shape[0]
    total = jnp.zeros((extent[0] * extent[1] * extent[2], row_count), jnp.float32)
    for tap_a in range(3):
        for tap_b in range(3):
            for tap_c in range(3):
                tap_index = tap_a * 9 + tap_b * 3 + tap_c
                view = tap_view(padded, tap_a, tap_b, tap_c, extent)
                total = total + lax.dot_general(
                    view,
                    block_rows[:, tap_index, :],
                    (((1,), (1,)), ((), ())),
                    preferred_element_type=jnp.float32,
                )
    return total.astype(jnp.bfloat16).reshape(extent[0], extent[1], extent[2], row_count)


def filter_terms(padded, flat_in, extent):
    pieces = []
    for tap_a in range(3):
        for tap_b in range(3):
            for tap_c in range(3):
                view = tap_view(padded, tap_a, tap_b, tap_c, extent)
                pieces.append(
                    lax.dot_general(
                        flat_in, view, (((0,), (0,)), ((), ())), preferred_element_type=jnp.float32
                    )
                )
    return jnp.stack(pieces, axis=1)


def on_device(raw_weight, inputs, cotangent):
    extent = inputs.shape[:3]
    channels = inputs.shape[3]
    shard_rows = raw_weight.shape[0]
    fan_count = channels * raw_weight.shape[1]
    padded = with_halo(cotangent, (("gx", 0), ("gy", 1), ("gz", 2)), 1)
    flat_in = inputs.reshape(-1, channels)
    whole_raw = lax.all_gather(raw_weight, ("gx", "gy"), axis=0, tiled=True)
    sum_first = jnp.sum(whole_raw, axis=(0, 1))
    sum_second = jnp.sum(whole_raw * whole_raw, axis=(0, 1))
    mean_out = sum_first / fan_count
    var_out = sum_second / fan_count - mean_out * mean_out
    inv_std = lax.rsqrt(var_out + var_eps)
    whole_std = (whole_raw - mean_out) * inv_std
    std_float = lax.dynamic_slice_in_dim(
        whole_std, lax.axis_index(("gx", "gy")) * shard_rows, shard_rows, 0
    )
    input_grad = input_rows(padded, extent, whole_std.astype(jnp.bfloat16))
    local_terms = filter_terms(padded, flat_in, extent)
    row_part = sent_and_summed(local_terms.astype(jnp.bfloat16), ("gx", "gy"), 0)
    filter_grad = of_everyone(row_part, "gz")
    local_grad = jnp.sum(filter_grad, axis=(0, 1))
    local_cross = jnp.sum(filter_grad * std_float, axis=(0, 1))
    local_square = jnp.sum(filter_grad * filter_grad, axis=(0, 1))
    sum_grad, sum_cross, sum_square = together(
        (local_grad, local_cross, local_square), ("gx", "gy")
    )
    mean_grad = sum_grad / fan_count
    mean_cross = sum_cross / fan_count
    raw_grad = inv_std * (filter_grad - mean_grad - std_float * mean_cross)
    per_output = sum_square - 2.0 * mean_grad * sum_grad - 2.0 * mean_cross * sum_cross
    per_output = (
        per_output
        + fan_count * mean_grad * mean_grad
        + fan_count * mean_cross * mean_cross * var_out / (var_out + var_eps)
    )
    square_sum = jnp.sum(inv_std * inv_std * per_output)
    scale = jnp.minimum(1.0, clip_norm * lax.rsqrt(square_sum + norm_eps))
    return (input_grad, raw_grad * scale)


def solution(mesh):
    in_specs = (P(("gx", "gy"), None, None), P("gx", "gy", "gz", None), P("gx", "gy", "gz", None))
    out_specs = (P("gx", "gy", "gz", None), P(("gx", "gy"), None, None))
    return jax.shard_map(
        on_device, mesh=mesh, in_specs=in_specs, out_specs=out_specs, check_vma=False
    )
```

profile of v0, /device:TPU:1, one launch (start us, length us, event | category | flops | bytes accessed | tf_op | source)
XLA Modules:
  0.0 167.2 jit_solution(6875055564060351250)
XLA Ops:
  7.2 0.9 fusion.71
  8.2 4.9 %collective-permute-start = (bf16[1,16,16,128]{3,2,1,0:T(8,128)(2,1)S(1)}, bf16[1,16,16,128]{3,2,1,0:T(8,128)(2,1)S(1)}, u32[]{:S(2)}, u32[]{:S(2)}) collective-permute-start(bf16[1,16,16,128]{3,2,1,0:T(8,128)(2,1)S(1)} %get-tuple-element.49), channel_id=1, source_target_pairs={{0,32},{32,64},{64,96},{96,128},{128,160},{160,192},{192,224},{1,3... | collective-permute-start | bytes 196616 | tf_op jit(solution)/shard_map/ppermute | solution.py:19
  13.1 1.9 %collective-permute-start.1 = (bf16[1,16,16,128]{3,2,1,0:T(8,128)(2,1)S(1)}, bf16[1,16,16,128]{3,2,1,0:T(8,128)(2,1)S(1)}, u32[]{:S(2)}, u32[]{:S(2)}) collective-permute-start(bf16[1,16,16,128]{3,2,1,0:T(8,128)(2,1)S(1)} %get-tuple-element.48), channel_id=1, source_target_pairs={{32,0},{64,32},{96,64},{128,96},{160,128},{192,160},{224,192},{33,... | collective-permute-start | bytes 196616 | tf_op jit(solution)/shard_map/ppermute | solution.py:21
  15.0 1.4 copy.131
  16.5 1.4 fusion.13
  18.0 0.4 constant_dynamic-update-slice_fusion.5
  18.7 3.2 %collective-permute-start.2 = (bf16[10,1,16,128]{3,2,1,0:T(8,128)(2,1)S(1)}, bf16[10,1,16,128]{3,2,1,0:T(8,128)(2,1)S(1)}, u32[]{:S(2)}, u32[]{:S(2)}) collective-permute-start(bf16[10,1,16,128]{3,2,1,0:T(8,128)(2,1)S(1)} %get-tuple-element.43), channel_id=1, source_target_pairs={{0,8},{8,16},{16,24},{1,9},{9,17},{17,25},{2,10},{10,18},{18,26},{... | collective-permute-start | bytes 122888 | tf_op jit(solution)/shard_map/ppermute | solution.py:19
  21.9 1.3 collective-permute-start.3
  24.0 2.7 %collective-permute-done.3 = bf16[10,1,16,128]{3,2,1,0:T(8,128)(2,1)S(1)} collective-permute-done((bf16[10,1,16,128]{3,2,1,0:T(8,128)(2,1)S(1)}, bf16[10,1,16,128]{3,2,1,0:T(8,128)(2,1)S(1)}, u32[]{:S(2)}, u32[]{:S(2)}) %collective-permute-start.3) | collective-permute-done | bytes 40992 | tf_op jit(solution)/shard_map/ppermute | solution.py:21
  26.8 1.3 collective-permute-start.4
  28.1 4.0 %collective-permute-start.5 = (bf16[10,18,1,128]{3,2,1,0:T(2,128)(2,1)S(1)}, bf16[10,18,1,128]{3,2,1,0:T(2,128)(2,1)S(1)}, u32[]{:S(2)}, u32[]{:S(2)}) collective-permute-start(bf16[10,18,1,128]{3,2,1,0:T(2,128)(2,1)S(1)} %get-tuple-element.33), channel_id=1, source_target_pairs={{0,1},{1,2},{2,3},{3,4},{4,5},{5,6},{6,7},{8,9},{9,10},{10,11},{11... | collective-permute-start | bytes 138248 | tf_op jit(solution)/shard_map/ppermute | solution.py:19
  34.3 0.8 pad_maximum_fusion.2
  35.2 0.4 fusion.4
  35.6 0.4 fusion.6
  36.7 0.4 fusion.8
  37.5 0.4 fusion.10
  38.3 0.4 fusion.12
  39.0 0.4 fusion.15
  39.8 0.4 fusion.17
  40.6 0.4 fusion.19
  41.3 0.4 fusion.21
  43.0 34.2 %all_to_all.16 = bf16[32,4,27,128]{3,1,2,0:T(4,128)(2,1)S(1)} all-to-all(bf16[32,4,27,128]{3,1,2,0:T(4,128)(2,1)S(1)} %constant_dynamic-update-slice_fusion.7), channel_id=1, replica_groups=mesh['gx'=8,'gy'=4,'gz'=8] {'gx','gy'}, dimensions={0} | all-to-all | bytes 1769472 | tf_op jit(solution)/shard_map/all_to_all | solution.py:36
  77.6 0.8 broadcast_in_dim.4
  78.4 15.7 %all-to-all-start.1 = ((f32[8,4,27,128]{3,1,2,0:T(4,128)}), f32[8,4,27,128]{3,1,2,0:T(4,128)}, u32[]{:S(2)}, u32[]{:S(2)}) async-start(f32[8,4,27,128]{3,1,2,0:T(4,128)} %broadcast_in_dim.4), calls=%async_computation.1 | async-start | bytes 884736 | tf_op jit(solution)/shard_map/all_to_all | solution.py:42
  94.1 2.0 %slice.311 = bf16[8,16,16,128]{3,2,1,0:T(8,128)(2,1)} slice(bf16[9,16,16,128]{3,2,1,0:T(8,128)(2,1)} %copy-done.2), slice={[1:9], [0:16], [0:16], [0:128]} | slice | bytes 1048576 | tf_op jit(solution)/shard_map/slice | solution.py:60
  96.1 0.8 slice.350
  97.0 1.7 %fusion.33 = (bf16[8,16,16,128]{3,2,1,0:T(8,128)(2,1)}, bf16[8,16,16,128]{3,2,1,0:T(8,128)(2,1)}, bf16[8,16,16,128]{3,2,1,0:T(8,128)(2,1)}, bf16[8,16,16,128]{3,...) fusion(bf16[10,1,16,128]{3,2,1,0:T(8,128)(2,1)S(1)} %collective-permute-done.2, ...), kind=kLoop, calls=%fused_computation.98 | loop fusion | flops 1572864 | bytes 3883008 | tf_op jit(solution)/shard_map/concatenate | solution.py:17
  98.7 3.9 %fusion.68 = (bf16[8,16,16,128]{3,2,1,0:T(8,128)(2,1)}, bf16[8,16,16,128]{3,2,1,0:T(8,128)(2,1)}, bf16[8,16,16,128]{3,2,1,0:T(8,128)(2,1)}, bf16[8,16,16,128]{3,...) fusion(bf16[10,18,17,128]{3,2,1,0:T(8,128)(2,1)S(1)} %get-tuple, ...), kind=kLoop, calls=%fused_computation.208 | loop fusion | bytes 18874368 | tf_op jit(solution)/shard_map/slice | solution.py:60
  102.6 4.1 %all-to-all-done.1 = f32[8,4,27,128]{3,1,2,0:T(4,128)} async-done(((f32[8,4,27,128]{3,1,2,0:T(4,128)}), f32[8,4,27,128]{3,1,2,0:T(4,128)}, u32[]{:S(2)}, u32[]{:S(2)}) %all-to-all-start.1) | async-done | bytes 442400 | tf_op jit(solution)/shard_map/all_to_all | solution.py:42
  106.7 1.3 fusion.65
  107.9 3.1 %all-gather.2.cloned.1.call-done = f32[128,27,128]{2,1,0:T(8,128)} async-done(((f32[4,27,128]{2,1,0:T(8,128)}), f32[128,27,128]{2,1,0:T(8,128)}) %all-gather.2.cloned.1.call-update) | async-done | bytes 1769488 | tf_op jit(solution)/shard_map/all_gather | solution.py:107
  111.0 2.3 %multiply_reduce_fusion = (f32[128]{0:T(128)S(1)}, f32[128]{0:T(128)S(1)}) fusion(f32[128,27,128]{2,1,0:T(8,128)} %all-gather.2.cloned.1.call-done), kind=kLoop, calls=%fused_computation.28 | loop fusion | flops 1326848 | bytes 1770496 | tf_op jit(solution)/shard_map/reduce_sum | solution.py:109
  113.3 1.1 fusion.66
  114.4 1.2 copy-done.33
  115.7 0.6 broadcast_in_dim.5
  116.4 13.6 %all-to-all-start.2 = ((f32[32,1,384]{2,1,0:T(1,128)}), f32[32,1,384]{2,1,0:T(1,128)S(1)}, u32[]{:S(2)}, u32[]{:S(2)}) async-start(f32[32,1,384]{2,1,0:T(1,128)} %broadcast_in_dim.5), calls=%async_computation.2 | async-start | bytes 98304 | tf_op jit(solution)/shard_map/all_to_all | solution.py:42
  130.6 0.7 copy-done.25
  131.6 0.7 copy-done.24
  132.7 0.7 copy-done.23
  133.7 0.7 copy-done.8
  134.8 0.7 copy-done.22
  135.8 0.7 copy-done.32
  136.8 0.7 copy-done.21
  137.9 0.7 copy-done.20
  138.9 0.7 copy-done.31
  140.0 0.7 copy-done.19
  141.0 0.7 copy-done.18
  142.1 0.7 copy-done.4
  143.1 0.7 copy-done.17
  144.1 0.7 copy-done.16
  145.2 0.7 copy-done.30
  146.2 0.7 copy-done.15
  147.3 0.7 copy-done.14
  148.3 0.7 copy-done.29
  149.4 0.7 copy-done.13
  150.4 0.7 copy-done.12
  151.4 0.7 copy-done.26
  152.5 0.7 copy-done.11
  153.5 0.7 copy-done.10
  154.6 0.7 copy-done.28
  155.6 0.7 copy-done.9
  156.3 1.1 fusion.2
  157.5 0.6 slice_multiply_fusion.1
  158.8 1.6 multiply_multiply_fusion
  (130 shorter events, 15.5 us)
Async XLA Ops:
  7.2 9.3 %copy-start = (bf16[8,16,16,128]{3,2,1,0:T(8,128)(2,1)S(1)}, bf16[8,16,16,128]{3,2,1,0:T(8,128)(2,1)}, u32[]{:S(2)}) copy-start(bf16[8,16,16,128]{3,2,1,0:T(8,128)(2,1)} %param.4) | copy-start | bytes 1572868
  7.2 103.8 %all-gather.2.cloned.1.call-start = ((), (), s32[]{:S(2)}) async-start(), calls=%async_computation.3 | async-start | bytes 2162688 | tf_op jit(solution)/shard_map/all_gather | solution.py:107
  8.2 9.8 %collective-permute-start = (bf16[1,16,16,128]{3,2,1,0:T(8,128)(2,1)S(1)}, bf16[1,16,16,128]{3,2,1,0:T(8,128)(2,1)S(1)}, u32[]{:S(2)}, u32[]{:S(2)}) collective-permute-start(bf16[1,16,16,128]{3,2,1,0:T(8,128)(2,1)S(1)} %get-tuple-element.49), channel_id=1, source_target_pairs={{0,32},{32,64},{64,96},{96,128},{128,160},{160,192},{192,224},{1,3... | collective-permute-start | bytes 196616 | tf_op jit(solution)/shard_map/ppermute | solution.py:19
  13.1 5.6 %collective-permute-start.1 = (bf16[1,16,16,128]{3,2,1,0:T(8,128)(2,1)S(1)}, bf16[1,16,16,128]{3,2,1,0:T(8,128)(2,1)S(1)}, u32[]{:S(2)}, u32[]{:S(2)}) collective-permute-start(bf16[1,16,16,128]{3,2,1,0:T(8,128)(2,1)S(1)} %get-tuple-element.48), channel_id=1, source_target_pairs={{32,0},{64,32},{96,64},{128,96},{160,128},{192,160},{224,192},{33,... | collective-permute-start | bytes 196616 | tf_op jit(solution)/shard_map/ppermute | solution.py:21
  16.5 1.5 copy-start.3
  18.4 5.5 %copy-start.5 = (bf16[9,16,16,128]{3,2,1,0:T(8,128)(2,1)}, bf16[9,16,16,128]{3,2,1,0:T(8,128)(2,1)S(1)}, u32[]{:S(2)}) copy-start(bf16[9,16,16,128]{3,2,1,0:T(8,128)(2,1)S(1)} %get-tuple-element.45) | copy-start | bytes 1769476
  18.7 5.3 %copy-start.2 = (bf16[9,16,16,128]{3,2,1,0:T(8,128)(2,1)}, bf16[9,16,16,128]{3,2,1,0:T(8,128)(2,1)S(1)}, u32[]{:S(2)}) copy-start(bf16[9,16,16,128]{3,2,1,0:T(8,128)(2,1)S(1)} %get-tuple-element.52) | copy-start | bytes 1769476
  18.7 5.2 %collective-permute-start.2 = (bf16[10,1,16,128]{3,2,1,0:T(8,128)(2,1)S(1)}, bf16[10,1,16,128]{3,2,1,0:T(8,128)(2,1)S(1)}, u32[]{:S(2)}, u32[]{:S(2)}) collective-permute-start(bf16[10,1,16,128]{3,2,1,0:T(8,128)(2,1)S(1)} %get-tuple-element.43), channel_id=1, source_target_pairs={{0,8},{8,16},{16,24},{1,9},{9,17},{17,25},{2,10},{10,18},{18,26},{... | collective-permute-start | bytes 122888 | tf_op jit(solution)/shard_map/ppermute | solution.py:19
  21.9 4.7 %collective-permute-start.3 = (bf16[10,1,16,128]{3,2,1,0:T(8,128)(2,1)S(1)}, bf16[10,1,16,128]{3,2,1,0:T(8,128)(2,1)S(1)}, u32[]{:S(2)}, u32[]{:S(2)}) collective-permute-start(bf16[10,1,16,128]{3,2,1,0:T(8,128)(2,1)S(1)} %get-tuple-element.44), channel_id=1, source_target_pairs={{8,0},{16,8},{24,16},{9,1},{17,9},{25,17},{10,2},{18,10},{26,18},{... | collective-permute-start | bytes 122888 | tf_op jit(solution)/shard_map/ppermute | solution.py:21
  26.8 7.4 %collective-permute-start.4 = (bf16[10,18,1,128]{3,2,1,0:T(2,128)(2,1)S(1)}, bf16[10,18,1,128]{3,2,1,0:T(2,128)(2,1)S(1)}, u32[]{:S(2)}, u32[]{:S(2)}) collective-permute-start(bf16[10,18,1,128]{3,2,1,0:T(2,128)(2,1)S(1)} %get-tuple-element.32), channel_id=1, source_target_pairs={{1,0},{2,1},{3,2},{4,3},{5,4},{6,5},{7,6},{9,8},{10,9},{11,10},{12... | collective-permute-start | bytes 138248 | tf_op jit(solution)/shard_map/ppermute | solution.py:21
  28.1 6.2 %collective-permute-start.5 = (bf16[10,18,1,128]{3,2,1,0:T(2,128)(2,1)S(1)}, bf16[10,18,1,128]{3,2,1,0:T(2,128)(2,1)S(1)}, u32[]{:S(2)}, u32[]{:S(2)}) collective-permute-start(bf16[10,18,1,128]{3,2,1,0:T(2,128)(2,1)S(1)} %get-tuple-element.33), channel_id=1, source_target_pairs={{0,1},{1,2},{2,3},{3,4},{4,5},{5,6},{6,7},{8,9},{9,10},{10,11},{11... | collective-permute-start | bytes 138248 | tf_op jit(solution)/shard_map/ppermute | solution.py:19
  78.4 28.2 %all-to-all-start.1 = ((f32[8,4,27,128]{3,1,2,0:T(4,128)}), f32[8,4,27,128]{3,1,2,0:T(4,128)}, u32[]{:S(2)}, u32[]{:S(2)}) async-start(f32[8,4,27,128]{3,1,2,0:T(4,128)} %broadcast_in_dim.4), calls=%async_computation.1 | async-start | bytes 884736 | tf_op jit(solution)/shard_map/all_to_all | solution.py:42
  94.1 2.0 %copy-start.6 = (bf16[9,16,16,128]{3,2,1,0:T(8,128)(2,1)S(1)}, bf16[9,16,16,128]{3,2,1,0:T(8,128)(2,1)}, u32[]{:S(2)}) copy-start(bf16[9,16,16,128]{3,2,1,0:T(8,128)(2,1)} %copy-done.5) | copy-start | bytes 1769476
  111.0 2.3 %copy-start.1 = (f32[128,27,128]{2,1,0:T(8,128)S(1)}, f32[128,27,128]{2,1,0:T(8,128)}, u32[]{:S(2)}) copy-start(f32[128,27,128]{2,1,0:T(8,128)} %all-gather.2.cloned.1.call-done) | copy-start | bytes 5308420
  113.3 16.6 %copy-start.27 = (bf16[8,16,16,128]{3,2,1,0:T(8,128)(2,1)S(1)}, bf16[8,16,16,128]{3,2,1,0:T(8,128)(2,1)}, u32[]{:S(2)}) copy-start(bf16[8,16,16,128]{3,2,1,0:T(8,128)(2,1)} %get-tuple-element.41) | copy-start | bytes 1572868
  114.4 1.2 copy-start.33
  114.4 15.9 %copy-start.7 = (bf16[8,16,16,128]{3,2,1,0:T(8,128)(2,1)S(1)}, bf16[8,16,16,128]{3,2,1,0:T(8,128)(2,1)}, u32[]{:S(2)}) copy-start(bf16[8,16,16,128]{3,2,1,0:T(8,128)(2,1)} %get-tuple-element.19) | copy-start | bytes 1572868
  116.4 41.1 %all-to-all-start.2 = ((f32[32,1,384]{2,1,0:T(1,128)}), f32[32,1,384]{2,1,0:T(1,128)S(1)}, u32[]{:S(2)}, u32[]{:S(2)}) async-start(f32[32,1,384]{2,1,0:T(1,128)} %broadcast_in_dim.5), calls=%async_computation.2 | async-start | bytes 98304 | tf_op jit(solution)/shard_map/all_to_all | solution.py:42
  130.3 1.0 copy-start.25
  131.3 1.0 copy-start.24
  132.4 1.0 copy-start.23
  133.4 1.0 copy-start.8
  134.5 1.0 copy-start.22
  135.5 1.0 copy-start.32
  136.5 1.0 copy-start.21
  137.6 1.0 copy-start.20
  138.6 1.0 copy-start.31
  139.7 1.0 copy-start.19
  140.7 1.0 copy-start.18
  141.8 1.0 copy-start.4
  142.8 1.0 copy-start.17
  143.8 1.0 copy-start.16
  144.9 1.0 copy-start.30
  145.9 1.0 copy-start.15
  147.0 1.0 copy-start.14
  148.0 1.0 copy-start.29
  149.1 1.0 copy-start.13
  150.1 1.0 copy-start.12
  151.1 1.0 copy-start.26
  152.2 1.0 copy-start.11
  153.2 1.0 copy-start.10
  154.3 1.0 copy-start.28
  155.3 1.0 copy-start.9
Sparse Core Ops, SparseCore 0:
  16.6 94.3 all-gather.1
where the time goes:
time: 169 us; the launch traced here: 167 us
  starting transfers between devices  46 us (27%)
  blocking collectives  34.2 us (20%)
  local copies, waits for them, and re-layouts  31.5 us (19%)
  matrix products  19.8 us (12%)
  between operations  15.5 us (9%)
  waiting for transfers between devices  10.2 us (6%)
  other arithmetic  10 us (6%)
    all_to_all x1, blocking collectives, sent_and_summed(): parts = lax.all_to_all(in_blocks(array, dim, peers), axis, 0, 0, tiled=True)  34.2 us
    all_to_all x2, starting transfers between devices, sent_to_all(): lax.all_to_all(jnp.broadcast_to(array[None], (peers, *array.shape)), axis...  29.3 us
    unnamed x97, local copies, waits for them, and re-layouts  21.9 us
    ppermute x3, starting transfers between devices, with_halo(): lax.ppermute(tail, axis, [(i, (i + 1) % count) for i in range(ends)])  12.1 us
    dot_general x27, matrix products, filter_terms(): lax.dot_general(flat_in, view, (((0,), (0,)), ((), ())), preferred_elemen...  11.1 us
    dot_general x27, matrix products, input_rows(): lax.dot_general(view, block_rows[:, tap_index, :], (((1,), (1,)), ((), ()...  8.72 us
    slice x3, local copies, waits for them, and re-layouts, tap_view(): padded[2 - tap_a:2 - tap_a + extent[0], 2 - tap_b:2 - tap_b + extent[1],...  6.69 us
    ppermute x3, starting transfers between devices, with_halo(): lax.ppermute(head, axis, [((i + 1) % count, i) for i in range(ends)])  4.5 us
  transfers between devices with their start and end apart: 9, of which 5 were waited for; matrix products, arithmetic and copies ran while one was open for 21% of the time, Pallas kernels for 0%

commit v1 on v0

v1 whole, which is shorter than its diff:
```python
import functools

import jax
import jax.numpy as jnp
from jax import lax
from jax.experimental import pallas as pl
from jax.experimental.pallas import tpu as pltpu
from jax.sharding import PartitionSpec as P

var_eps = 1e-05
norm_eps = 1e-06
clip_norm = 600.0

f32 = jnp.float32
bf16 = jnp.bfloat16
MESH = pl.DeviceIdType.MESH

C = 128
LX, LY, LZ = 8, 16, 16
CELLS = LX * LY * LZ
PITCH = 32
FAN = 27 * C

TAPS = [(ab // 3, ab % 3, c) for c in (1, 0, 2) for ab in range(9)]
WIDTH_TAPS = (1, 0, 2)
CHUNKS = ((0, 2), (2, 5), (5, 7))
DIRECTIONS = [
    (dx, dy, dz)
    for dz in (-1, 1, 0)
    for dx in (0, -1, 1)
    for dy in (0, -1, 1)
    if (dx, dy, dz) != (0, 0, 0)
]


def body(raw_ref, x_ref, cot_ref, dx_ref, dw_ref, full, pad, zface, zedge, zhalo, zcorner, xt,
         rawp, raws, part, w, own, psend, precv, spread, r1, red, r2, rows, gath, nat, stat,
         hs, hr, ws, wr, fs, fr, ds, dr, s1, q1, s2, q2, s3, q3, s4, q4):
    gx, gy, gz = lax.axis_index("gx"), lax.axis_index("gy"), lax.axis_index("gz")
    z_lo, core = gx // 2, gx % 2
    z_hi, x = gz // 4, gz % 4
    z = z_hi * 4 + z_lo
    mine = gy * 4 + x
    full2 = full.reshape(10 * 18 * PITCH, C)

    def dev(a, b, c):
        return (a, b, c)

    def gx_peer(k):
        return dev((gx + k) % 8, gy, gz)

    def chip_peer(k):
        return dev(((z_lo + k) % 4) * 2 + core, gy, gz)

    def gy_peer(k):
        return dev(gx, (gy + k) % 4, gz)

    def x_peer(k):
        return dev(gx, gy, z_hi * 4 + (x + k) % 4)

    def xy_peer(k):
        return dev(gx, (gy + k // 4) % 4, z_hi * 4 + (x + k % 4) % 4)

    def z_peer(k):
        zz = (z + k) % 8
        return dev((zz % 4) * 2 + core, gy, (zz // 4) * 4 + x)

    def plane_peer(k):
        return dev((gx + k // 4) % 8, (gy + k % 4) % 4, gz)

    partner = dev(gx + 1 - 2 * core, gy, gz)

    def remote(src, dst, send, recv, device):
        return pltpu.make_async_remote_copy(
            src_ref=src, dst_ref=dst, send_sem=send, recv_sem=recv, device_id=device, device_id_type=MESH
        )

    def drain(ref, sem):
        pltpu.make_async_copy(ref, ref, sem).wait()

    def exists(axis_index, last, step):
        if step == 0:
            return None
        return axis_index > 0 if step < 0 else axis_index < last

    def present(d):
        tests = [exists(gx, 7, d[0]), exists(gy, 3, d[1]), exists(gz, 7, d[2])]
        tests = [t for t in tests if t is not None]
        out = tests[0]
        for t in tests[1:]:
            out = jnp.logical_and(out, t)
        return out

    barrier = pltpu.get_barrier_semaphore()

    def greet(device):
        pl.semaphore_signal(barrier, inc=1, device_id=device, device_id_type=MESH)

    wide = [d for d in DIRECTIONS if d[2] != 0]
    greeted = jnp.int32(0)
    for d in wide:
        there = present(d)

        @pl.when(there)
        def _(d=d):
            greet(dev(gx + d[0], gy + d[1], gz + d[2]))

        greeted = greeted + there.astype(jnp.int32)
    lax.fori_loop(1, 8, lambda k, _: (greet(z_peer(k)), 0)[1], 0)
    lax.fori_loop(1, 16, lambda k, _: (greet(xy_peer(k)), 0)[1], 0)
    lax.fori_loop(1, 32, lambda k, _: (greet(plane_peer(k)), 0)[1], 0)

    def fill(i, _):
        slab = cot_ref[i]
        pad[1, i + 1, 1 : LY + 1] = slab
        full[i + 1, 1 : LY + 1, 8 : 8 + LZ, :] = slab.astype(f32)
        return 0

    lax.fori_loop(0, LX, fill, 0)

    def faces(i, _):
        for s, zr in ((0, 8), (1, 8 + LZ - 1)):
            zface[s, i] = full2[pl.ds(((i + 1) * 18 + 1) * PITCH + zr, LY, stride=PITCH), :].astype(bf16)
        return 0

    lax.fori_loop(0, LX, faces, 0)
    for s, zr in ((0, 8), (1, 8 + LZ - 1)):
        for e, yr in ((0, 1), (1, LY)):
            for i in range(LX):
                at = ((i + 1) * 18 + yr) * PITCH + zr
                zedge[s, e, i : i + 1, :] = full2[at : at + 1, :]
    for r in range(4):
        rawp[r * 32 : r * 32 + 27, :] = raw_ref[r]
        rawp[r * 32 + 27 : r * 32 + 32, :] = jnp.zeros((5, C), f32)
    raws[gy] = rawp[...]

    tile = jnp.zeros((LZ, C), bf16)

    @pl.when(gx == 0)
    def _():
        for j in range(18):
            pad[1, 0, j] = tile

    @pl.when(gx == 7)
    def _():
        for j in range(18):
            pad[1, 9, j] = tile

    @pl.when(gy == 0)
    def _():
        for i in range(10):
            pad[1, i, 0] = tile

    @pl.when(gy == 3)
    def _():
        for i in range(10):
            pad[1, i, 17] = tile

    for s, gone in ((0, gz == 0), (1, gz == 7)):

        @pl.when(gone)
        def _(s=s):
            for i in range(10):
                zhalo[s, i] = tile
            for e in range(2):
                for k in range(3):
                    zcorner[s, e, k] = jnp.zeros((8, C), f32)

        @pl.when(jnp.logical_and(jnp.logical_not(gone), gx == 0))
        def _(s=s):
            zhalo[s, 0] = tile
            for e in range(2):
                zcorner[s, e, 0] = jnp.zeros((8, C), f32)

        @pl.when(jnp.logical_and(jnp.logical_not(gone), gx == 7))
        def _(s=s):
            zhalo[s, 9] = tile
            for e in range(2):
                zcorner[s, e, 2] = jnp.zeros((8, C), f32)

        for e, lost in ((0, gy == 0), (1, gy == 3)):

            @pl.when(jnp.logical_and(jnp.logical_not(gone), lost))
            def _(s=s, e=e):
                for k in range(3):
                    zcorner[s, e, k] = jnp.zeros((8, C), f32)

    pl.semaphore_wait(barrier, greeted + (7 + 15 + 31))

    def halo_copy(n, d):
        dx, dy, dz = d
        xs, xd = (None, None) if dx == 0 else ((0, 9) if dx < 0 else (LX - 1, 0))
        ys, yd = (None, None) if dy == 0 else ((0, 17) if dy < 0 else (LY - 1, 0))
        if dz == 0:
            if dy == 0:
                src, dst = cot_ref.at[xs], pad.at[1, xd, pl.ds(1, LY)]
            elif dx == 0:
                src, dst = cot_ref.at[:, ys], pad.at[1, pl.ds(1, LX), yd]
            else:
                src, dst = cot_ref.at[xs, ys], pad.at[1, xd, yd]
        else:
            s = 0 if dz < 0 else 1
            r = 1 - s
            if dy == 0:
                if dx == 0:
                    src, dst = zface.at[s], zhalo.at[r, pl.ds(1, LX)]
                else:
                    src, dst = zface.at[s, xs], zhalo.at[r, xd]
            else:
                e = 0 if dy < 0 else 1
                k = 1 if dx == 0 else (2 if dx < 0 else 0)
                src, dst = zedge.at[s, e], zcorner.at[r, 1 - e, k]
        return remote(src, dst, hs.at[n], hr.at[n], dev(gx + dx, gy + dy, gz + dz))

    for n, d in enumerate(DIRECTIONS):

        @pl.when(present(d))
        def _(n=n, d=d):
            halo_copy(n, d).start()

    def halo_wait(flat):
        for n, d in enumerate(DIRECTIONS):
            if (d[2] == 0) == flat:

                @pl.when(present((-d[0], -d[1], -d[2])))
                def _(n=n, d=d):
                    halo_copy(n, d).wait_recv()

    def to_gy(k, _):
        remote(rawp, raws.at[gy], ws.at[0], wr.at[0], gy_peer(k)).start()
        return 0

    lax.fori_loop(1, 4, to_gy, 0)

    m = lax.broadcasted_iota(jnp.int32, (C, C), 0)
    col = lax.broadcasted_iota(jnp.int32, (C, C), 1)
    want = (m % 4) * 32 + (m // 4 + 16 * core) % 32
    order = jnp.where(col == want, 1.0, 0.0).astype(bf16)
    for j in range(4):
        xt[:, j * 512 : (j + 1) * 512] = lax.dot_general(
            order,
            x_ref[2 * j : 2 * j + 2].reshape(512, C),
            (((1,), (1,)), ((), ())),
            preferred_element_type=f32,
        ).astype(bf16)

    drain(raws.at[pl.ds(0, 3)], wr.at[0])
    first = jnp.zeros((1, C), f32)
    second = jnp.zeros((1, C), f32)
    for j in range(4):
        v = raws[j]
        first = first + jnp.sum(v, axis=0, keepdims=True)
        second = second + jnp.sum(v * v, axis=0, keepdims=True)
    row = lax.broadcasted_iota(jnp.int32, (8, C), 0)
    part[gx] = jnp.where(row == 0, first, jnp.where(row == 1, second, 0.0))

    def to_gx(k, _):
        remote(part.at[gx], part.at[gx], ws.at[1], wr.at[1], gx_peer(k)).start()
        return 0

    lax.fori_loop(1, 8, to_gx, 0)

    def quad(q):
        outs = []
        for h in range(2):
            views = []
            for p in (4 * q + 2 * h, 4 * q + 2 * h + 1):
                if p < 27:
                    a, b, c = TAPS[p]
                    views.append(pad[c, 2 - a : 2 - a + LX, 2 - b : 2 - b + LY].reshape(CELLS, C))
            v = jnp.concatenate(views, axis=1) if len(views) == 2 else views[0]
            o = jnp.dot(xt[...], v, preferred_element_type=f32)
            outs.append(o[:, :C])
            outs.append(o[:, C:] if len(views) == 2 else jnp.zeros((C, C), f32))
        low = lax.broadcasted_iota(jnp.int32, (16, 8, C), 1) < 4
        pieces = [[], []]
        for h in range(2):
            one = outs[2 * h].reshape(16, 8, C)
            two = outs[2 * h + 1].reshape(16, 8, C)
            pieces[0].append(jnp.where(low, one, pltpu.roll(two, 4, 1)))
            pieces[1].append(jnp.where(low, pltpu.roll(one, 4, 1), two))
        for e in range(2):
            t = jnp.concatenate(pieces[e], axis=1)
            for j in range(8):
                own[q, 2 * j + e] = t[j]
                psend[q, 2 * j + e] = t[8 + j].astype(bf16)
        remote(psend.at[q], precv.at[q], ds.at[q], dr.at[q], partner).start()

    def spread_chunk(n):
        lo, hi = CHUNKS[n]
        for q in range(lo, hi):
            drain(precv.at[q], dr.at[q])

            def mix(d, _, q=q):
                spread[d, q] = (own[q, d] + precv[q, d].astype(f32)).astype(bf16)
                return 0

            lax.fori_loop(0, 16, mix, 0, unroll=4)

        def send(k, _):
            there = ((gy + k // 4) % 4) * 4 + (x + k % 4) % 4
            remote(
                spread.at[there, pl.ds(lo, hi - lo)],
                r1.at[k - 1, pl.ds(lo, hi - lo)],
                s1.at[n],
                q1.at[n],
                xy_peer(k),
            ).start()
            return 0

        lax.fori_loop(1, 16, send, 0)

    halo_wait(True)
    quad(0)
    quad(1)

    drain(part.at[pl.ds(0, 7)], wr.at[1])
    total = part[0]
    for j in range(1, 8):
        total = total + part[j]
    mean = total[0:1] / FAN
    var = total[1:2] / FAN - mean * mean
    inv = lax.rsqrt(var + var_eps)
    raws2 = raws.reshape(512, C)
    mine_rows = pl.ds(pl.multiple_of(gx * 16, 16), 16)
    for p in range(27):
        a, b, c = TAPS[p]
        t = 9 * a + 3 * b + c
        v = raws2[pl.ds(t, 16, stride=32), :]
        w[mine_rows, p * C : (p + 1) * C] = ((v - mean) * inv).astype(bf16)

    def slab(g):
        return w.at[pl.ds(pl.multiple_of(g * 16, 16), 16)]

    def to_z(k, _):
        remote(slab(gx), slab(gx), ws.at[2], wr.at[2], chip_peer(k)).start()
        return 0

    lax.fori_loop(1, 4, to_z, 0)
    remote(slab(gx), slab(gx), fs.at[0], fr.at[0], partner).start()

    for i in (0, 9):
        full[i, :, 8 : 8 + LZ, :] = pad[1, i].astype(f32)
    for j in (0, 17):
        full[1 : LX + 1, j, 8 : 8 + LZ, :] = pad[1, 1 : LX + 1, j].astype(f32)
    spread_chunk(0)
    halo_wait(False)
    for s, zr in ((0, 7), (1, 8 + LZ)):

        def put(i, _, s=s, zr=zr):
            full2[pl.ds((i * 18 + 1) * PITCH + zr, LY, stride=PITCH), :] = zhalo[s, i].astype(f32)
            return 0

        lax.fori_loop(0, 10, put, 0)
        for e, yr in ((0, 0), (1, 17)):
            for i in range(10):
                at = (i * 18 + yr) * PITCH + zr
                k, r = (1, i - 1) if 0 < i < 9 else ((0, 7) if i == 0 else (2, 0))
                full2[at : at + 1, :] = zcorner[s, e, k, r : r + 1, :]

    def shift(i, _):
        pad[0, i] = full[i, :, 9 : 9 + LZ, :].astype(bf16)
        pad[2, i] = full[i, :, 7 : 7 + LZ, :].astype(bf16)
        return 0

    lax.fori_loop(0, 10, shift, 0)
    for q in range(2, 5):
        quad(q)
    quad(5)
    spread_chunk(1)
    quad(6)

    drain(w.at[pl.ds(0, 48)], wr.at[2])
    spread_chunk(2)

    def hand_on(k, _):
        g = ((z_lo + k) % 4) * 2 + core
        remote(slab(g), slab(g), fs.at[1], fr.at[1], partner).start()
        return 0

    lax.fori_loop(1, 4, hand_on, 0)

    def input_grad(i0, count):
        def one(i, _):
            views = []
            for a, b, c in TAPS:
                v = pad[c, pl.ds(2 * i + 2 - a, 2), 2 - b : 2 - b + LY]
                views.append(v.reshape(2 * LY * LZ, C))
            out = lax.dot_general(
                jnp.concatenate(views, axis=1), w[...], (((1,), (1,)), ((), ())), preferred_element_type=f32
            )
            dx_ref[pl.ds(2 * i, 2)] = out.astype(bf16).reshape(2, LY, LZ, C)
            return 0

        lax.fori_loop(i0, i0 + count, one, 0)

    for n in range(3):
        lo, hi = CHUNKS[n]
        drain(r1.at[:, pl.ds(lo, hi - lo)], q1.at[n])
    for q in range(7):
        acc = own[q, mine] + precv[q, mine].astype(f32)
        for k in range(15):
            acc = acc + r1[k, q].astype(f32)
        red[q * 16 : (q + 1) * 16, :] = acc
    red[112:128, :] = jnp.zeros((16, C), f32)
    for j in range(4):
        rows[j] = red[pl.ds(j, 32, stride=4), :].astype(bf16)
    r2[z] = rows[z_lo]

    def to_all_z(k, _):
        remote(rows.at[(z_lo + k) % 4], r2.at[z], s2.at[0], q2.at[0], z_peer(k)).start()
        return 0

    lax.fori_loop(1, 8, to_all_z, 0)

    drain(w.at[pl.ds(0, 16)], fr.at[0])
    drain(w.at[pl.ds(0, 48)], fr.at[1])
    input_grad(0, 2)

    drain(r2.at[pl.ds(0, 7)], q2.at[0])
    acc = r2[0].astype(f32)
    for j in range(1, 8):
        acc = acc + r2[j].astype(f32)
    gath[x] = acc

    def to_x(k, _):
        remote(gath.at[x], gath.at[x], s3.at[0], q3.at[0], x_peer(k)).start()
        return 0

    lax.fori_loop(1, 4, to_x, 0)
    input_grad(2, 1)

    drain(gath.at[pl.ds(0, 3)], q3.at[0])
    for r in range(4):
        for n, c in enumerate(WIDTH_TAPS):
            nat[pl.ds(r * 32 + c, 9, stride=3), :] = gath[r, n * 9 : n * 9 + 9, :]
    g_first = jnp.zeros((1, C), f32)
    g_cross = jnp.zeros((1, C), f32)
    g_second = jnp.zeros((1, C), f32)
    for r in range(4):
        g = nat[r * 32 : r * 32 + 27, :]
        std = (raw_ref[r] - mean) * inv
        g_first = g_first + jnp.sum(g, axis=0, keepdims=True)
        g_cross = g_cross + jnp.sum(g * std, axis=0, keepdims=True)
        g_second = g_second + jnp.sum(g * g, axis=0, keepdims=True)
    stat[gx * 4 + gy] = jnp.where(
        row == 0, g_first, jnp.where(row == 1, g_cross, jnp.where(row == 2, g_second, 0.0))
    )

    def to_plane(k, _):
        here = stat.at[gx * 4 + gy]
        remote(here, here, s4.at[0], q4.at[0], plane_peer(k)).start()
        return 0

    lax.fori_loop(1, 32, to_plane, 0)
    input_grad(3, 1)
    drain(stat.at[pl.ds(0, 31)], q4.at[0])
    total = stat[0]
    for j in range(1, 32):
        total = total + stat[j]
    sum_grad, sum_cross, sum_square = total[0:1], total[1:2], total[2:3]
    mean_grad = sum_grad / FAN
    mean_cross = sum_cross / FAN
    per_output = sum_square - 2.0 * mean_grad * sum_grad - 2.0 * mean_cross * sum_cross
    per_output = (
        per_output + FAN * mean_grad * mean_grad + FAN * mean_cross * mean_cross * var / (var + var_eps)
    )
    square_sum = jnp.sum(inv * inv * per_output, axis=1, keepdims=True)
    scale = jnp.minimum(1.0, clip_norm * lax.rsqrt(square_sum + norm_eps))
    for r in range(4):
        g = nat[r * 32 : r * 32 + 27, :]
        std = (raw_ref[r] - mean) * inv
        dw_ref[r] = inv * (g - mean_grad - std * mean_cross) * scale

    for n, d in enumerate(DIRECTIONS):

        @pl.when(present(d))
        def _(n=n, d=d):
            halo_copy(n, d).wait_send()

    drain(raws.at[pl.ds(0, 3)], ws.at[0])
    drain(part.at[pl.ds(0, 7)], ws.at[1])
    drain(w.at[pl.ds(0, 48)], ws.at[2])
    drain(w.at[pl.ds(0, 16)], fs.at[0])
    drain(w.at[pl.ds(0, 48)], fs.at[1])
    for q in range(7):
        drain(precv.at[q], ds.at[q])
    for n in range(3):
        lo, hi = CHUNKS[n]
        drain(r1.at[:, pl.ds(lo, hi - lo)], s1.at[n])
    drain(r2.at[pl.ds(0, 7)], s2.at[0])
    drain(gath.at[pl.ds(0, 3)], s3.at[0])
    drain(stat.at[pl.ds(0, 31)], s4.at[0])


def on_device(raw_weight, inputs, cotangent):
    dma = pltpu.SemaphoreType.DMA
    vmem = pltpu.VMEM
    return pl.pallas_call(
        body,
        out_shape=(
            jax.ShapeDtypeStruct(inputs.shape, bf16),
            jax.ShapeDtypeStruct(raw_weight.shape, f32),
        ),
        in_specs=[pl.BlockSpec(memory_space=pltpu.VMEM)] * 3,
        out_specs=[pl.BlockSpec(memory_space=pltpu.VMEM)] * 2,
        scratch_shapes=[
            vmem((10, 18, PITCH, C), f32),
            vmem((3, 10, 18, LZ, C), bf16),
            vmem((2, LX, LY, C), bf16),
            vmem((2, 2, 8, C), f32),
            vmem((2, 10, LY, C), bf16),
            vmem((2, 2, 3, 8, C), f32),
            vmem((C, CELLS), bf16),
            vmem((128, C), f32),
            vmem((4, 128, C), f32),
            vmem((8, 8, C), f32),
            vmem((C, 27 * C), bf16),
            vmem((7, 16, 16, C), f32),
            vmem((7, 16, 16, C), bf16),
            vmem((7, 16, 16, C), bf16),
            vmem((16, 7, 16, C), bf16),
            vmem((15, 7, 16, C), bf16),
            vmem((128, C), f32),
            vmem((8, 32, C), bf16),
            vmem((4, 32, C), bf16),
            vmem((4, 32, C), f32),
            vmem((128, C), f32),
            vmem((32, 8, C), f32),
            dma((26,)), dma((26,)),
            dma((3,)), dma((3,)),
            dma((2,)), dma((2,)),
            dma((7,)), dma((7,)),
            dma((3,)), dma((3,)),
            dma((1,)), dma((1,)),
            dma((1,)), dma((1,)),
            dma((1,)), dma((1,)),
        ],
        compiler_params=pltpu.CompilerParams(
            collective_id=0, has_side_effects=True, vmem_limit_bytes=40 * 1024 * 1024
        ),
    )(raw_weight, inputs, cotangent)


def solution(mesh):
    in_specs = (P(("gx", "gy"), None, None), P("gx", "gy", "gz", None), P("gx", "gy", "gz", None))
    out_specs = (P("gx", "gy", "gz", None), P(("gx", "gy"), None, None))
    return jax.shard_map(
        on_device, mesh=mesh, in_specs=in_specs, out_specs=out_specs, check_vma=False
    )
```

time: 169 us -> 58 us (0.34)
  Pallas kernels: 0 us -> 52.8 us
  starting transfers between devices: 46 us -> 0 us
  blocking collectives: 34.2 us -> 0 us
  local copies, waits for them, and re-layouts: 31.5 us -> 4.36 us
  matrix products: 19.8 us -> 0 us
  between operations: 15.5 us -> 0.64 us
  waiting for transfers between devices: 10.2 us -> 0 us
  other arithmetic: 10 us -> 0 us
    pallas_call x0 -> x1, Pallas kernels: none -> 52.8 us  [on_device(): pl.pallas_call(body, out_shape=(jax.ShapeDtypeStruct(inputs.shape, bf16),...]
    all_to_all x1 -> x0, blocking collectives: 34.2 us -> none  [sent_and_summed(): parts = lax.all_to_all(in_blocks(array, dim, peers), axis, 0, 0, tiled=True)]
    all_to_all x2 -> x0, starting transfers between devices: 29.3 us -> none  [sent_to_all(): lax.all_to_all(jnp.broadcast_to(array[None], (peers, *array.shape)), axis...]
    dot_general x54 -> x0, matrix products: 19.8 us -> none  [the longest x27 11.1 us: filter_terms(): lax.dot_general(flat_in, view, (((0,), (0,)), ((), ())), preferred_elemen...]
    unnamed x97 -> x6, local copies, waits for them, and re-layouts: 21.9 us -> 3.7 us
    ppermute x6 -> x0, starting transfers between devices: 16.6 us -> none  [the longest x3 12.1 us: with_halo(): lax.ppermute(tail, axis, [(i, (i + 1) % count) for i in range(ends)])]
    slice x5 -> x0, local copies, waits for them, and re-layouts: 7.63 us -> none  [the longest x3 6.69 us: tap_view(): padded[2 - tap_a:2 - tap_a + extent[0], 2 - tap_b:2 - tap_b + extent[1],...]
    all_to_all x2 -> x0, waiting for transfers between devices: 4.08 us -> none  [sent_to_all(): lax.all_to_all(jnp.broadcast_to(array[None], (peers, *array.shape)), axis...]
  transfers between devices with their start and end apart: 9 -> 0, of which waited for: 5 -> 0; matrix products, arithmetic and copies ran while one was open for 21% -> 0% of each run, Pallas kernels for 0% -> 0%
where the time goes in v1:
time: 58 us; the launch traced here: 57.8 us
  Pallas kernels  52.8 us (91%)
  local copies, waits for them, and re-layouts  4.36 us (8%)
  between operations  0.64 us (1%)
    pallas_call x1, Pallas kernels, on_device(): pl.pallas_call(body, out_shape=(jax.ShapeDtypeStruct(inputs.shape, bf16),...  52.8 us
    unnamed x6, local copies, waits for them, and re-layouts  3.7 us

profile of v1, /device:TPU:1, one launch (start us, length us, event | category | flops | bytes accessed | tf_op | source)
XLA Modules:
  0.0 57.8 jit_solution(14893819824333880846)
XLA Ops:
  0.6 0.8 %copy.5.raw_ref = f32[4,27,128]{2,1,0:T(8,128)S(1)} copy(f32[4,27,128]{2,0,1:T(4,128)} %param.3) | data formatting | bytes 110592 | tf_op args[0]
  1.4 0.0 copy-start
  1.5 1.0 %copy-done = bf16[8,16,16,128]{3,2,1,0:T(8,128)(2,1)S(1)} copy-done((bf16[8,16,16,128]{3,2,1,0:T(8,128)(2,1)S(1)}, bf16[8,16,16,128]{3,2,1,0:T(8,128)(2,1)}, u32[]{:S(2)}) %copy-start) | copy-done | bytes 524312
  2.5 0.0 copy-start.1
  2.5 1.0 %copy-done.1 = bf16[8,16,16,128]{3,2,1,0:T(8,128)(2,1)S(1)} copy-done((bf16[8,16,16,128]{3,2,1,0:T(8,128)(2,1)S(1)}, bf16[8,16,16,128]{3,2,1,0:T(8,128)(2,1)}, u32[]{:S(2)}) %copy-start.1) | copy-done | bytes 524312
  3.5 52.8 %shard_map.50 = (bf16[8,16,16,128]{3,2,1,0:T(8,128)(2,1)S(1)}, f32[4,27,128]{2,1,0:T(8,128)S(1)}) custom-call(f32[4,27,128]{2,1,0:T(8,128)S(1)} %copy.5.raw_ref, bf16[8,16,16,128]{3,2,1,0:T(8,128)(2,1)S(1)} %copy-done, bf16[8,16,16,128]{3,2,1,0:T(8,128)(2,1)S(1)} %copy-done.1), custom_call_target="tpu_custom_call" | custom-call | tf_op jit(solution)/shard_map/pallas_call | solution.py:499
  56.3 0.7 %copy.6 = f32[4,27,128]{2,0,1:T(4,128)} copy(f32[4,27,128]{2,1,0:T(8,128)S(1)} %get-tuple-element.3) | data formatting | bytes 110592 | tf_op jit(solution)/shard_map/pallas_call | solution.py:499
  57.0 0.8 %copy.8 = bf16[8,16,16,128]{3,2,1,0:T(8,128)(2,1)} copy(bf16[8,16,16,128]{3,2,1,0:T(8,128)(2,1)S(1)} %get-tuple-element.6) | data formatting | bytes 1048576
Async XLA Ops:
  1.4 1.0 %copy-start = (bf16[8,16,16,128]{3,2,1,0:T(8,128)(2,1)S(1)}, bf16[8,16,16,128]{3,2,1,0:T(8,128)(2,1)}, u32[]{:S(2)}) copy-start(bf16[8,16,16,128]{3,2,1,0:T(8,128)(2,1)} %x_ref.1) | copy-start | bytes 1572868
  2.5 1.0 %copy-start.1 = (bf16[8,16,16,128]{3,2,1,0:T(8,128)(2,1)S(1)}, bf16[8,16,16,128]{3,2,1,0:T(8,128)(2,1)}, u32[]{:S(2)}) copy-start(bf16[8,16,16,128]{3,2,1,0:T(8,128)(2,1)} %cot_ref.1) | copy-start | bytes 1572868

commit v2 on v1

v2 whole, which is shorter than its diff:
```python
import functools

import jax
import jax.numpy as jnp
from jax import lax
from jax.experimental import pallas as pl
from jax.experimental.pallas import tpu as pltpu
from jax.sharding import PartitionSpec as P

var_eps = 1e-05
norm_eps = 1e-06
clip_norm = 600.0

f32 = jnp.float32
bf16 = jnp.bfloat16
MESH = pl.DeviceIdType.MESH

C = 128
LX, LY, LZ = 8, 16, 16
CELLS = LX * LY * LZ
PITCH = 32
FAN = 27 * C

TAPS = [(t // 9, t // 3 % 3, t % 3) for t in range(27)]
CHUNKS = ((0, 2), (2, 4), (4, 7))
DIRECTIONS = [
    (dx, dy, dz)
    for dz in (-1, 1, 0)
    for dx in (0, -1, 1)
    for dy in (0, -1, 1)
    if (dx, dy, dz) != (0, 0, 0)
]


def body(raw_hbm, x_hbm, cot_hbm, dx_ref, dw_ref, raw_ref, x_ref, cot_ref,
         full, pad, zface, zedge, zpoint, zhalo, zcorner, zdot, plane, turned, xf, xt, xz, base,
         raws, mine_raw, part, w, wt, part_dx, own, psend, precv, spread, r1, red, comp, r2, rows, gath, nat, mine_std, stat,
         ls, hr, wr, dr, ours, got, sent):
    gx, gy, gz = lax.axis_index("gx"), lax.axis_index("gy"), lax.axis_index("gz")
    def div(a, n):
        return lax.div(a, jnp.int32(n))

    def mod(a, n):
        return lax.rem(a, jnp.int32(n))

    z_lo, core = div(gx, 2), mod(gx, 2)
    z_hi, x = div(gz, 4), mod(gz, 4)
    z = z_hi * 4 + z_lo
    mine = gy * 4 + x
    early_tap, late_tap = 2 - 2 * z_hi, 2 * z_hi
    early_side, late_side = z_hi, 1 - z_hi
    full2 = full.reshape(10 * 18 * PITCH, C)

    def dev(a, b, c):
        return (a, b, c)

    def ring(step):
        zz = mod(z + step, 8)
        return mod(zz, 4), div(zz, 4)

    spots = [ring(step) for step in range(8)] + [ring(2 + 4 * core)]
    at_gz = [hi * 4 + x for _, hi in spots]
    at_gx = [[lo * 2 + core, lo * 2 + 1 - core] for lo, _ in spots]
    at_gy = [gy] + [mod(gy + k, 4) for k in range(1, 4)]
    at_x = [x] + [mod(x + k, 4) for k in range(1, 4)]
    x_gz = [gz] + [z_hi * 4 + at_x[k] for k in range(1, 4)]

    def chip_peer(step):
        return dev(at_gx[step][0], gy, at_gz[step])

    def gy_peer(k):
        return dev(gx, at_gy[k], gz)

    def x_peer(k):
        return dev(gx, gy, x_gz[k])

    def xy_peer(k):
        return dev(gx, at_gy[k // 4], x_gz[k % 4])

    z_peer = chip_peer
    def plane_peer(k, step):
        return dev(at_gx[step][k // 4], at_gy[k % 4], at_gz[step])

    def to_plane(send, steps=(2, 1, 7, 0)):
        for step in steps:
            for k in range(1 if step == 0 else 0, 8):
                send(plane_peer(k, step))

    partner = dev(gx + 1 - 2 * core, gy, gz)

    def remote(src, dst, recv, device):
        return pltpu.make_async_remote_copy(
            src_ref=src, dst_ref=dst, send_sem=sent.at[0], recv_sem=recv, device_id=device, device_id_type=MESH
        )

    def rows_wait(n, sem):
        view = full2.at[pl.ds(0, n)]
        pltpu.make_async_copy(view, view, sem).wait()

    def drain(ref, sem):
        pltpu.make_async_copy(ref, ref, sem).wait()

    def exists(axis_index, last, step):
        if step == 0:
            return None
        return axis_index > 0 if step < 0 else axis_index < last

    def count(axis_index, last):
        return (axis_index > 0).astype(jnp.int32) + (axis_index < last).astype(jnp.int32)

    def present(d):
        tests = [exists(gx, 7, d[0]), exists(gy, 3, d[1]), exists(gz, 7, d[2])]
        tests = [t for t in tests if t is not None]
        out = tests[0]
        for t in tests[1:]:
            out = jnp.logical_and(out, t)
        return out

    loads = [
        pltpu.make_async_copy(a, b, ls.at[n])
        for n, (a, b) in enumerate(((cot_hbm, cot_ref), (raw_hbm, raw_ref), (x_hbm, x_ref)))
    ]
    for load in loads:
        load.start()

    barrier = pltpu.get_barrier_semaphore()

    def greet(device):
        pl.semaphore_signal(barrier, inc=1, device_id=device, device_id_type=MESH)

    wide = [d for d in DIRECTIONS if d[2] != 0]
    greeted = jnp.int32(0)
    for d in wide:
        there = present(d)

        @pl.when(there)
        def _(d=d):
            greet(dev(gx + d[0], gy + d[1], gz + d[2]))

        greeted = greeted + there.astype(jnp.int32)
    for k in (4, 3, 5, 2):
        greet(z_peer(k))
    for k in (10, 11, 9, 6, 14, 5, 7, 13, 15, 1, 2, 3):
        greet(xy_peer(k))
    to_plane(greet, (6, 1, 7, 0))

    loads[0].wait()

    def fill(i, _):
        slab = cot_ref[i]
        pad[1, i + 1, 1 : LY + 1] = slab
        full[i + 1, 1 : LY + 1, 8 : 8 + LZ, :] = slab.astype(f32)
        return 0

    lax.fori_loop(0, LX, fill, 0)

    def faces(i, _):
        for s, zr in ((0, 8), (1, 8 + LZ - 1)):
            zface[s, i] = full2[pl.ds(((i + 1) * 18 + 1) * PITCH + zr, LY, stride=PITCH), :].astype(bf16)
        return 0

    lax.fori_loop(0, LX, faces, 0)
    for s, zr in ((0, 8), (1, 8 + LZ - 1)):
        for e, yr in ((0, 1), (1, LY)):
            for i in range(LX):
                at = ((i + 1) * 18 + yr) * PITCH + zr
                zedge[s, e, i : i + 1, :] = full2[at : at + 1, :]
            zpoint[s, e, 0] = zedge[s, e, 0:1, :]
            zpoint[s, e, 1] = zedge[s, e, LX - 1 : LX, :]
    for i in range(10):
        for zr in (7, 8 + LZ):
            full2[pl.ds(i * 18 * PITCH + zr, 18, stride=PITCH), :] = jnp.zeros((18, C), f32)
    loads[1].wait()
    raws[gy] = raw_ref[...]
    first = jnp.zeros((4, C), f32)
    second = jnp.zeros((4, C), f32)
    for t in range(27):
        v = raw_ref[t]
        first = first + v
        second = second + v * v
    part[gx * 4 + gy, 0:1, :] = jnp.sum(first, axis=0, keepdims=True)
    part[gx * 4 + gy, 1:2, :] = jnp.sum(second, axis=0, keepdims=True)

    tile = jnp.zeros((LZ, C), bf16)

    @pl.when(gx == 0)
    def _():
        for j in range(18):
            pad[1, 0, j] = tile

    @pl.when(gx == 7)
    def _():
        for j in range(18):
            pad[1, 9, j] = tile

    @pl.when(gy == 0)
    def _():
        for i in range(10):
            pad[1, i, 0] = tile

    @pl.when(gy == 3)
    def _():
        for i in range(10):
            pad[1, i, 17] = tile

    for r, z_there in ((0, gz > 0), (1, gz < 7)):

        @pl.when(jnp.logical_not(z_there))
        def _(r=r):
            for i in range(10):
                zhalo[r, i] = tile

        for k, x_there in ((0, gx > 0), (1, gx < 7)):

            @pl.when(jnp.logical_and(z_there, jnp.logical_not(x_there)))
            def _(r=r, k=k):
                zhalo[r, 9 * k] = tile

        for e, y_there in ((0, gy > 0), (1, gy < 3)):
            both = jnp.logical_and(z_there, y_there)

            @pl.when(jnp.logical_not(both))
            def _(r=r, e=e):
                zcorner[r, e] = jnp.zeros((8, C), f32)

            for k, x_there in ((0, gx > 0), (1, gx < 7)):

                @pl.when(jnp.logical_not(jnp.logical_and(both, x_there)))
                def _(r=r, e=e, k=k):
                    zdot[r, e, k] = jnp.zeros((1, C), f32)

    pl.semaphore_wait(barrier, greeted + (4 + 12 + 31))

    def halo_copy(d):
        dx, dy, dz = d
        xs, xd = (None, None) if dx == 0 else ((0, 9) if dx < 0 else (LX - 1, 0))
        ys, yd = (None, None) if dy == 0 else ((0, 17) if dy < 0 else (LY - 1, 0))
        if dz == 0:
            if dy == 0:
                src, dst = cot_ref.at[xs], pad.at[1, xd, pl.ds(1, LY)]
            elif dx == 0:
                src, dst = cot_ref.at[:, ys], pad.at[1, pl.ds(1, LX), yd]
            else:
                src, dst = cot_ref.at[xs, ys], pad.at[1, xd, yd]
        else:
            s = 0 if dz < 0 else 1
            r = 1 - s
            if dy == 0:
                if dx == 0:
                    src, dst = zface.at[s], zhalo.at[r, pl.ds(1, LX)]
                else:
                    src, dst = zface.at[s, xs], zhalo.at[r, xd]
            else:
                e = 0 if dy < 0 else 1
                if dx == 0:
                    src, dst = zedge.at[s, e], zcorner.at[r, 1 - e]
                elif dx < 0:
                    src, dst = zpoint.at[s, e, 0], zdot.at[r, 1 - e, 1]
                else:
                    src, dst = zpoint.at[s, e, 1], zdot.at[r, 1 - e, 0]
        return remote(src, dst, hr.at[0 if dz == 0 else (2 if dz < 0 else 1)], dev(gx + dx, gy + dy, gz + dz))

    def send_part(device):
        here = part.at[gx * 4 + gy]
        remote(here, here, wr.at[1], device).start()

    to_plane(send_part)
    for d in DIRECTIONS:

        @pl.when(present(d))
        def _(d=d):
            halo_copy(d).start()

    near_x, near_y, near_z = count(gx, 7), count(gy, 3), count(gz, 7)

    def flat_rows(nx, ny):
        return 128 * nx + 64 * ny + 8 * nx * ny

    def wide_rows(nx, ny):
        return 64 + 8 * nx + 8 * ny + nx * ny

    def by_neighbours(rows, sem):
        for nx in (1, 2):
            for ny in (1, 2):

                @pl.when(jnp.logical_and(near_x == nx, near_y == ny))
                def _(nx=nx, ny=ny):
                    rows_wait(rows(nx, ny), sem)

    def wide_wait(late):
        for half in (0, 1):
            there = z_hi == half
            if not late:
                there = jnp.logical_and(there, near_z == 2)

            @pl.when(there)
            def _(half=half):
                by_neighbours(wide_rows, hr.at[1 + (1 - half if late else half)])

    for k in (2, 1, 3):
        remote(raw_ref, raws.at[gy], wr.at[0], gy_peer(k)).start()


    loads[2].wait()
    m = lax.broadcasted_iota(jnp.int32, (C, C), 0)
    col = lax.broadcasted_iota(jnp.int32, (C, C), 1)
    want = (m % 4) * 32 + (m // 4 + 16 * core) % 32
    order = jnp.where(col == want, 1.0, 0.0).astype(bf16)
    for j in range(4):
        xt[:, j * 512 : (j + 1) * 512] = lax.dot_general(
            order,
            x_ref[2 * j : 2 * j + 2].reshape(512, C),
            (((1,), (1,)), ((), ())),
            preferred_element_type=f32,
        ).astype(bf16)

    def widen(i, _):
        xf[pl.ds(pl.multiple_of(i * LY * LZ, LY * LZ), LY * LZ), :] = x_ref[i].reshape(LY * LZ, C).astype(f32)
        return 0

    lax.fori_loop(0, LX, widen, 0)
    xz[...] = lax.dot_general(
        order,
        xf[pl.ds(late_side * (LZ - 1), LX * LY, stride=LZ), :].astype(bf16),
        (((1,), (1,)), ((), ())),
        preferred_element_type=f32,
    ).astype(bf16)

    def tap_of(p):
        return p % 9 // 3, p % 3, (1, early_tap, late_tap)[p // 9]

    def pair_main(q, h):
        views = []
        for p in (4 * q + 2 * h, 4 * q + 2 * h + 1):
            if p < 27:
                a, b, c = tap_of(p)
                views.append(pad[c, 2 - a : 2 - a + LX, 2 - b : 2 - b + LY].reshape(CELLS, C))
        v = jnp.concatenate(views, axis=1) if len(views) == 2 else views[0]
        o = jnp.dot(xt[...], v, preferred_element_type=f32)
        return o if len(views) == 2 else jnp.concatenate([o, jnp.zeros((C, C), f32)], axis=1)

    def pair_rest(q, h):
        views = []
        for p in (4 * q + 2 * h, 4 * q + 2 * h + 1):
            if p < 27:
                a, b, _ = tap_of(p)
                views.append(turned[b, 2 - a : 2 - a + LX].reshape(LX * LY, C))
            else:
                views.append(jnp.zeros((LX * LY, C), bf16))
        return jnp.dot(xz[...], jnp.concatenate(views, axis=1), preferred_element_type=f32)

    def main(q):
        for h in range(2):
            base[2 * (q - 4) + h] = pair_main(q, h)

    def quad(q):
        outs = []
        for h in range(2):
            if q < 4:
                o = pair_main(q, h)
            else:
                o = base[2 * (q - 4) + h]
                if 4 * q + 2 * h >= 18:
                    o = o + pair_rest(q, h)
            outs += [o[:, :C], o[:, C:]]
        low = lax.broadcasted_iota(jnp.int32, (16, 8, C), 1) < 4
        pieces = [[], []]
        for h in range(2):
            one = outs[2 * h].reshape(16, 8, C)
            two = outs[2 * h + 1].reshape(16, 8, C)
            pieces[0].append(jnp.where(low, one, pltpu.roll(two, 4, 1)))
            pieces[1].append(jnp.where(low, pltpu.roll(one, 4, 1), two))
        for e in range(2):
            t = jnp.concatenate(pieces[e], axis=1)
            for j in range(8):
                own[q, 2 * j + e] = t[j]
                psend[q, 2 * j + e] = t[8 + j].astype(bf16)

    def quads(n):
        lo, hi = CHUNKS[n]
        for q in range(lo, hi):
            quad(q)
        some = pl.ds(lo, hi - lo)
        remote(psend.at[some], precv.at[some], dr.at[n], partner).start()

    def spread_chunk(n):
        lo, hi = CHUNKS[n]
        drain(precv.at[pl.ds(lo, hi - lo)], dr.at[n])
        for q in range(lo, hi):
            spread[:, q] = (own[q] + precv[q].astype(f32)).astype(bf16)

        for k in (10, 11, 9, 6, 14, 2, 8, 5, 7, 13, 15, 1, 3, 4, 12):
            remote(
                spread.at[at_gy[k // 4] * 4 + at_x[k % 4], pl.ds(lo, hi - lo)],
                r1.at[k - 1, pl.ds(lo, hi - lo)],
                got.at[1],
                xy_peer(k),
            ).start()

    by_neighbours(flat_rows, hr.at[0])
    quads(0)

    def lay_out(side):
        for i in range(10):
            plane[side, i, 8 : 8 + LY, :] = zhalo[side, i].astype(f32)
            for e, yr in ((0, 7), (1, 8 + LY)):
                if 0 < i < 9:
                    plane[side, i, yr : yr + 1, :] = zcorner[side, e, i - 1 : i, :]
                else:
                    plane[side, i, yr : yr + 1, :] = zdot[side, e, i // 9]

    def put_in(side):
        zr = 7 + 17 * side

        def put(i, _):
            full2[pl.ds(i * 18 * PITCH + zr, 18, stride=PITCH), :] = plane[side, i, 7 : 7 + 18, :]
            return 0

        lax.fori_loop(0, 10, put, 0)

    wide_wait(False)

    lay_out(early_side)
    put_in(early_side)
    for i in (0, 9):
        full[i, :, 8 : 8 + LZ, :] = pad[1, i].astype(f32)
    for j in (0, 17):
        full[1 : LX + 1, j, 8 : 8 + LZ, :] = pad[1, 1 : LX + 1, j].astype(f32)

    def shift(i, _):
        pad[0, i] = full[i, :, 9 : 9 + LZ, :].astype(bf16)
        pad[2, i] = full[i, :, 7 : 7 + LZ, :].astype(bf16)
        return 0

    lax.fori_loop(0, 10, shift, 0)
    quads(1)
    spread_chunk(0)
    for q in range(4, 7):
        main(q)
    drain(part.at[pl.ds(0, 31)], wr.at[1])
    drain(raws.at[pl.ds(0, 3)], wr.at[0])
    total = part[0]
    for j in range(1, 32):
        total = total + part[j]
    mean = total[0:1] / FAN
    var = total[1:2] / FAN - mean * mean
    inv = lax.rsqrt(var + var_eps)
    for t in range(27):
        for j in range(4):
            mine_raw[t, 4 * j : 4 * j + 4, :] = raws[j, t]
    mine_rows = pl.ds(pl.multiple_of(gx * 16, 16), 16)
    for p in range(27):
        a, b, c = TAPS[p]
        t = 9 * a + 3 * b + c
        w[mine_rows, p * C : (p + 1) * C] = ((mine_raw[t] - mean) * inv).astype(bf16)
    for t in range(27):
        mine_std[4 * t : 4 * t + 4, :] = (raw_ref[t] - mean) * inv

    halves = (slice(0, 14 * C), slice(14 * C, 27 * C))

    def slab(g, h):
        return w.at[pl.ds(pl.multiple_of(g * 16, 16), 16), halves[h]]

    for h in range(2):
        for step in (8, 1, 7):
            remote(slab(gx, h), slab(gx, h), wr.at[2 + h], chip_peer(step)).start()
    for h in range(2):
        remote(slab(gx, h), slab(gx, h), ours.at[h], partner).start()

    spread_chunk(1)
    wide_wait(True)
    lay_out(late_side)
    for i in range(10):
        turned[1, i] = zhalo[late_side, i]
        for b in (0, 2):
            turned[b, i] = plane[late_side, i, 9 - b : 9 - b + LY, :].astype(bf16)
    quads(2)
    spread_chunk(2)
    def hand_on(h):
        drain(w.at[pl.ds(0, 48), halves[h]], wr.at[2 + h])
        for k in (1, 2, 3):
            g = at_gx[k][0]
            remote(slab(g, h), slab(g, h), ours.at[h], partner).start()

    def take_over(h):
        drain(w.at[pl.ds(0, 64), halves[h]], ours.at[h])
        for p in range(14 * h, 14 + 13 * h):
            wt[p * C : (p + 1) * C, :] = w[:, p * C : (p + 1) * C].T

    def input_grad(h, lo, hi):
        def one(i, _):
            views = []
            for a, b, c in TAPS[14 * h : 14 + 13 * h]:
                views.append(pad[c, i + 2 - a, 2 - b : 2 - b + LY].reshape(LY * LZ, C))
            out = jnp.dot(jnp.concatenate(views, axis=1), wt[halves[h], :], preferred_element_type=f32)
            if h == 0:
                part_dx[i] = out
            else:
                dx_ref[i] = (part_dx[i] + out).astype(bf16).reshape(LY, LZ, C)
            return 0

        lax.fori_loop(lo, hi, one, 0)

    put_in(late_side)
    lax.fori_loop(0, 10, shift, 0)
    drain(r1, got.at[1])
    for q in range(7):
        acc = own[q, mine] + precv[q, mine].astype(f32)
        for k in range(15):
            acc = acc + r1[k, q].astype(f32)
        red[q * 16 : (q + 1) * 16, :] = acc
    for j in range(4):
        for n, start in enumerate((0, 72 - 36 * z_hi, 36 + 36 * z_hi)):
            comp[j, 9 * n : 9 * n + 9, :] = red[pl.ds(start + j, 9, stride=4), :]
        comp[j, 27:32, :] = jnp.zeros((5, C), f32)
        rows[j] = comp[j].astype(bf16)
    r2[z] = rows[z_lo]

    for k in (4, 3, 5, 2, 6, 1, 7):
        remote(rows.at[spots[k][0]], r2.at[z], got.at[2], z_peer(k)).start()

    hand_on(0)
    take_over(0)
    input_grad(0, 0, 8)
    hand_on(1)
    drain(r2.at[pl.ds(0, 7)], got.at[2])
    acc = r2[0].astype(f32)
    for j in range(1, 8):
        acc = acc + r2[j].astype(f32)
    gath[x] = acc

    for k in (2, 1, 3):
        remote(gath.at[x], gath.at[x], got.at[3], x_peer(k)).start()
    take_over(1)
    input_grad(1, 0, 4)

    drain(gath.at[pl.ds(0, 3)], got.at[3])
    for r in range(4):
        for n, c in enumerate((1, 0, 2)):
            nat[pl.ds(4 * c + r, 9, stride=12), :] = gath[r, n * 9 : n * 9 + 9, :]
    g = nat[0:108, :]
    std = mine_std[0:108, :]
    here = gx * 4 + gy
    stat[here, 0:1, :] = jnp.sum(g, axis=0, keepdims=True)
    stat[here, 1:2, :] = jnp.sum(g * std, axis=0, keepdims=True)
    stat[here, 2:3, :] = jnp.sum(g * g, axis=0, keepdims=True)
    stat[here, 3:4, :] = jnp.zeros((1, C), f32)

    def send_stat(device):
        remote(stat.at[here], stat.at[here], got.at[4], device).start()

    to_plane(send_stat)
    input_grad(1, 4, 8)
    drain(stat.at[pl.ds(0, 31)], got.at[4])
    total = stat[0]
    for j in range(1, 32):
        total = total + stat[j]
    sum_grad, sum_cross, sum_square = total[0:1], total[1:2], total[2:3]
    mean_grad = sum_grad / FAN
    mean_cross = sum_cross / FAN
    per_output = sum_square - 2.0 * mean_grad * sum_grad - 2.0 * mean_cross * sum_cross
    per_output = (
        per_output + FAN * mean_grad * mean_grad + FAN * mean_cross * mean_cross * var / (var + var_eps)
    )
    square_sum = jnp.sum(inv * inv * per_output, axis=1, keepdims=True)
    scale = jnp.minimum(1.0, clip_norm * lax.rsqrt(square_sum + norm_eps))
    factor = inv * scale
    for t in range(27):
        g = nat[4 * t : 4 * t + 4, :]
        dw_ref[t] = factor * (g - mean_grad - mine_std[4 * t : 4 * t + 4, :] * mean_cross)

    always = (3 * 27 * 4 * C + 31 * 2 * C + 31 * 4 * C + 3 * 32 * C) * 4 + (
        7 * 16 * 27 * C + 7 * 256 * C + 15 * 112 * C + 7 * 32 * C
    ) * 2
    for nz in (1, 2):

        @pl.when(near_z == nz)
        def _(nz=nz):
            by_neighbours(
                lambda nx, ny: flat_rows(nx, ny) + nz * wide_rows(nx, ny) + always // (4 * C), sent.at[0]
            )


def hand_over(dx_in, dw_in, dx_out, dw_out, sems):
    copies = [
        pltpu.make_async_copy(a, b, sems.at[n]) for n, (a, b) in enumerate(((dx_in, dx_out), (dw_in, dw_out)))
    ]
    for copy in copies:
        copy.start()
    for copy in copies:
        copy.wait()


def on_device(raw_weight, inputs, cotangent):
    dma = pltpu.SemaphoreType.DMA
    vmem = pltpu.VMEM
    dx, dw = pl.pallas_call(
        body,
        out_shape=(
            pltpu.VMEM(inputs.shape, bf16),
            pltpu.VMEM((27, 4, C), f32),
        ),
        in_specs=[pl.BlockSpec(memory_space=pltpu.HBM)] * 3,
        out_specs=[pl.BlockSpec(memory_space=pltpu.VMEM)] * 2,
        scratch_shapes=[
            vmem((27, 4, C), f32),
            vmem((LX, LY, LZ, C), bf16),
            vmem((LX, LY, LZ, C), bf16),
            vmem((10, 18, PITCH, C), f32),
            vmem((3, 10, 18, LZ, C), bf16),
            vmem((2, LX, LY, C), bf16),
            vmem((2, 2, 8, C), f32),
            vmem((2, 2, 2, 1, C), f32),
            vmem((2, 10, LY, C), bf16),
            vmem((2, 2, 8, C), f32),
            vmem((2, 2, 2, 1, C), f32),
            vmem((2, 10, 32, C), f32),
            vmem((3, 10, LY, C), bf16),
            vmem((CELLS, C), f32),
            vmem((C, CELLS), bf16),
            vmem((C, C), bf16),
            vmem((6, C, 2 * C), f32),
            vmem((4, 27, 4, C), f32),
            vmem((27, 16, C), f32),
            vmem((32, 2, C), f32),
            vmem((C, 27 * C), bf16),
            vmem((27 * C, C), bf16),
            vmem((LX, LY * LZ, C), f32),
            vmem((7, 16, 16, C), f32),
            vmem((7, 16, 16, C), bf16),
            vmem((7, 16, 16, C), bf16),
            vmem((16, 7, 16, C), bf16),
            vmem((15, 7, 16, C), bf16),
            vmem((112, C), f32),
            vmem((4, 32, C), f32),
            vmem((8, 32, C), bf16),
            vmem((4, 32, C), bf16),
            vmem((4, 32, C), f32),
            vmem((112, C), f32),
            vmem((112, C), f32),
            vmem((32, 4, C), f32),
            dma((3,)),
            dma((3,)),
            dma((4,)),
            dma((3,)),
            dma((2,)),
            dma((5,)),
            dma((1,)),
        ],
        compiler_params=pltpu.CompilerParams(
            collective_id=0, has_side_effects=True, vmem_limit_bytes=40 * 1024 * 1024
        ),
    )(*[pltpu.with_memory_space_constraint(a, pltpu.HBM) for a in (jnp.swapaxes(raw_weight, 0, 1), inputs, cotangent)])
    dx, dw = pl.pallas_call(
        hand_over,
        out_shape=(jax.ShapeDtypeStruct(dx.shape, bf16), jax.ShapeDtypeStruct(dw.shape, f32)),
        in_specs=[pl.BlockSpec(memory_space=pltpu.VMEM)] * 2,
        out_specs=[pl.BlockSpec(memory_space=pl.ANY)] * 2,
        scratch_shapes=[dma((2,))],
    )(*[pltpu.with_memory_space_constraint(a, pltpu.VMEM) for a in (dx, dw)])
    return dx, jnp.swapaxes(dw, 0, 1)


def solution(mesh):
    in_specs = (P(("gx", "gy"), None, None), P("gx", "gy", "gz", None), P("gx", "gy", "gz", None))
    out_specs = (P("gx", "gy", "gz", None), P(("gx", "gy"), None, None))
    return jax.shard_map(
        on_device, mesh=mesh, in_specs=in_specs, out_specs=out_specs, check_vma=False
    )
```

time: 58 us -> 42.2 us (0.73)
  Pallas kernels: 52.8 us -> 41.5 us
  local copies, waits for them, and re-layouts: 4.36 us -> 0 us
    pallas_call x1 -> x2, Pallas kernels: 52.8 us -> 41.5 us  [the longest x1 40.7 us: on_device(): pl.pallas_call(body, out_shape=(pltpu.VMEM(inputs.shape, bf16), pltpu.VME...]
    unnamed x6 -> x0, local copies, waits for them, and re-layouts: 3.7 us -> none
    pallas_call x1 -> x0, local copies, waits for them, and re-layouts: 0.66 us -> none  [on_device(): pl.pallas_call(body, out_shape=(jax.ShapeDtypeStruct(inputs.shape, bf16),...]
where the time goes in v2:
time: 42.2 us; the launch traced here: 42.1 us
  Pallas kernels  41.5 us (98%)
  between operations  0.64 us (2%)
    pallas_call x1, Pallas kernels, on_device(): pl.pallas_call(body, out_shape=(pltpu.VMEM(inputs.shape, bf16), pltpu.VME...  40.7 us

profile of v2, /device:TPU:1, one launch (start us, length us, event | category | flops | bytes accessed | tf_op | source)
XLA Modules:
  0.0 42.1 jit_solution(14964779276883304302)
XLA Ops:
  0.6 40.7 %shard_map.50 = (bf16[8,16,16,128]{3,2,1,0:T(8,128)(2,1)S(1)}, f32[27,4,128]{2,1,0:T(4,128)S(1)}) custom-call(f32[27,4,128]{2,1,0:T(4,128)} %bitcast.2, bf16[8,16,16,128]{3,2,1,0:T(8,128)(2,1)} %x_hbm.1, bf16[8,16,16,128]{3,2,1,0:T(8,128)(2,1)} %cot_hbm.1), custom_call_target="tpu_custom_call" | custom-call | tf_op jit(solution)/shard_map/pallas_call | solution.py:597
  41.3 0.8 %shard_map.51 = (bf16[8,16,16,128]{3,2,1,0:T(8,128)(2,1)}, f32[27,4,128]{2,1,0:T(4,128)}) custom-call(bf16[8,16,16,128]{3,2,1,0:T(8,128)(2,1)S(1)} %get-tuple-element.6.dx_in, f32[27,4,128]{2,1,0:T(4,128)S(1)} %get-tuple-element.7.dw_in), custom_call_target="tpu_custom_call" | custom-call | tf_op jit(solution)/shard_map/pallas_call | solution.py:654

commit v3 on v2

--- a/solution.py
+++ b/solution.py
@@ -33,7 +33,7 @@
 
 
 def body(raw_hbm, x_hbm, cot_hbm, dx_ref, dw_ref, raw_ref, x_ref, cot_ref,
-         full, pad, zface, zedge, zpoint, zhalo, zcorner, zdot, plane, turned, xf, xt, xz, base,
+         full, pad, zface, zedge, zpoint, zhalo, zcorner, zdot, plane, turned, xf, xt, xy, xz, grad, land_x, land_y, land_c,
          raws, mine_raw, part, w, wt, part_dx, own, psend, precv, spread, r1, red, comp, r2, rows, gath, nat, mine_std, stat,
          ls, hr, wr, dr, ours, got, sent):
     gx, gy, gz = lax.axis_index("gx"), lax.axis_index("gy"), lax.axis_index("gz")
@@ -167,9 +167,6 @@
                 zedge[s, e, i : i + 1, :] = full2[at : at + 1, :]
             zpoint[s, e, 0] = zedge[s, e, 0:1, :]
             zpoint[s, e, 1] = zedge[s, e, LX - 1 : LX, :]
-    for i in range(10):
-        for zr in (7, 8 + LZ):
-            full2[pl.ds(i * 18 * PITCH + zr, 18, stride=PITCH), :] = jnp.zeros((18, C), f32)
     loads[1].wait()
     raws[gy] = raw_ref[...]
     first = jnp.zeros((4, C), f32)
@@ -181,67 +178,19 @@
     part[gx * 4 + gy, 0:1, :] = jnp.sum(first, axis=0, keepdims=True)
     part[gx * 4 + gy, 1:2, :] = jnp.sum(second, axis=0, keepdims=True)
 
-    tile = jnp.zeros((LZ, C), bf16)
-
-    @pl.when(gx == 0)
-    def _():
-        for j in range(18):
-            pad[1, 0, j] = tile
-
-    @pl.when(gx == 7)
-    def _():
-        for j in range(18):
-            pad[1, 9, j] = tile
-
-    @pl.when(gy == 0)
-    def _():
-        for i in range(10):
-            pad[1, i, 0] = tile
-
-    @pl.when(gy == 3)
-    def _():
-        for i in range(10):
-            pad[1, i, 17] = tile
-
-    for r, z_there in ((0, gz > 0), (1, gz < 7)):
-
-        @pl.when(jnp.logical_not(z_there))
-        def _(r=r):
-            for i in range(10):
-                zhalo[r, i] = tile
-
-        for k, x_there in ((0, gx > 0), (1, gx < 7)):
-
-            @pl.when(jnp.logical_and(z_there, jnp.logical_not(x_there)))
-            def _(r=r, k=k):
-                zhalo[r, 9 * k] = tile
-
-        for e, y_there in ((0, gy > 0), (1, gy < 3)):
-            both = jnp.logical_and(z_there, y_there)
-
-            @pl.when(jnp.logical_not(both))
-            def _(r=r, e=e):
-                zcorner[r, e] = jnp.zeros((8, C), f32)
-
-            for k, x_there in ((0, gx > 0), (1, gx < 7)):
-
-                @pl.when(jnp.logical_not(jnp.logical_and(both, x_there)))
-                def _(r=r, e=e, k=k):
-                    zdot[r, e, k] = jnp.zeros((1, C), f32)
-
     pl.semaphore_wait(barrier, greeted + (4 + 12 + 31))
 
     def halo_copy(d):
         dx, dy, dz = d
-        xs, xd = (None, None) if dx == 0 else ((0, 9) if dx < 0 else (LX - 1, 0))
-        ys, yd = (None, None) if dy == 0 else ((0, 17) if dy < 0 else (LY - 1, 0))
+        xs, xd = (None, None) if dx == 0 else ((0, 1) if dx < 0 else (LX - 1, 0))
+        ys, yd = (None, None) if dy == 0 else ((0, 1) if dy < 0 else (LY - 1, 0))
         if dz == 0:
             if dy == 0:
-                src, dst = cot_ref.at[xs], pad.at[1, xd, pl.ds(1, LY)]
+                src, dst = cot_ref.at[xs], land_x.at[xd]
             elif dx == 0:
-                src, dst = cot_ref.at[:, ys], pad.at[1, pl.ds(1, LX), yd]
+                src, dst = cot_ref.at[:, ys], land_y.at[yd]
             else:
-                src, dst = cot_ref.at[xs, ys], pad.at[1, xd, yd]
+                src, dst = cot_ref.at[xs, ys], land_c.at[xd, yd]
         else:
             s = 0 if dz < 0 else 1
             r = 1 - s
@@ -249,7 +198,7 @@
                 if dx == 0:
                     src, dst = zface.at[s], zhalo.at[r, pl.ds(1, LX)]
                 else:
-                    src, dst = zface.at[s, xs], zhalo.at[r, xd]
+                    src, dst = zface.at[s, xs], zhalo.at[r, 9 * xd]
             else:
                 e = 0 if dy < 0 else 1
                 if dx == 0:
@@ -264,7 +213,6 @@
         here = part.at[gx * 4 + gy]
         remote(here, here, wr.at[1], device).start()
 
-    to_plane(send_part)
     for d in DIRECTIONS:
 
         @pl.when(present(d))
@@ -299,8 +247,80 @@
 
     for k in (2, 1, 3):
         remote(raw_ref, raws.at[gy], wr.at[0], gy_peer(k)).start()
-
-
+    to_plane(send_part)
+
+    tile = jnp.zeros((LZ, C), bf16)
+
+    for c in range(3):
+        for i in (0, 9):
+            for j in range(18):
+                pad[c, i, j] = tile
+        for i in range(1, 9):
+            pad[c, i, 0] = tile
+            pad[c, i, 17] = tile
+
+    for k, x_there in ((0, gx > 0), (1, gx < 7)):
+
+        @pl.when(jnp.logical_not(x_there))
+        def _(k=k):
+            for j in range(LY):
+                land_x[k, j] = tile
+
+        for e, y_there in ((0, gy > 0), (1, gy < 3)):
+
+            @pl.when(jnp.logical_not(jnp.logical_and(x_there, y_there)))
+            def _(k=k, e=e):
+                land_c[k, e] = tile
+
+    for e, y_there in ((0, gy > 0), (1, gy < 3)):
+
+        @pl.when(jnp.logical_not(y_there))
+        def _(e=e):
+            for i in range(LX):
+                land_y[e, i] = tile
+
+    for r, z_there in ((0, gz > 0), (1, gz < 7)):
+
+        @pl.when(jnp.logical_not(z_there))
+        def _(r=r):
+            for i in range(10):
+                zhalo[r, i] = tile
+
+        for k, x_there in ((0, gx > 0), (1, gx < 7)):
+
+            @pl.when(jnp.logical_and(z_there, jnp.logical_not(x_there)))
+            def _(r=r, k=k):
+                zhalo[r, 9 * k] = tile
+
+        for e, y_there in ((0, gy > 0), (1, gy < 3)):
+            both = jnp.logical_and(z_there, y_there)
+
+            @pl.when(jnp.logical_not(both))
+            def _(r=r, e=e):
+                zcorner[r, e] = jnp.zeros((8, C), f32)
+
+            for k, x_there in ((0, gx > 0), (1, gx < 7)):
+
+                @pl.when(jnp.logical_not(jnp.logical_and(both, x_there)))
+                def _(r=r, e=e, k=k):
+                    zdot[r, e, k] = jnp.zeros((1, C), f32)
+
+    for i in range(10):
+        for zr in (7, 8 + LZ):
+            full2[pl.ds(i * 18 * PITCH + zr, 18, stride=PITCH), :] = jnp.zeros((18, C), f32)
+
+    def shift(i, _):
+        pad[0, i] = full[i, :, 9 : 9 + LZ, :].astype(bf16)
+        pad[2, i] = full[i, :, 7 : 7 + LZ, :].astype(bf16)
+        return 0
+
+    def shift_inside(i, _):
+        inside = slice(1, LY + 1)
+        pad[0, i, inside] = full[i, inside, 9 : 9 + LZ, :].astype(bf16)
+        pad[2, i, inside] = full[i, inside, 7 : 7 + LZ, :].astype(bf16)
+        return 0
+
+    lax.fori_loop(1, LX + 1, shift_inside, 0)
     loads[2].wait()
     m = lax.broadcasted_iota(jnp.int32, (C, C), 0)
     col = lax.broadcasted_iota(jnp.int32, (C, C), 1)
@@ -319,50 +339,34 @@
         return 0
 
     lax.fori_loop(0, LX, widen, 0)
-    xz[...] = lax.dot_general(
-        order,
-        xf[pl.ds(late_side * (LZ - 1), LX * LY, stride=LZ), :].astype(bf16),
-        (((1,), (1,)), ((), ())),
-        preferred_element_type=f32,
-    ).astype(bf16)
+    def by_channel(cells):
+        return lax.dot_general(order, cells, (((1,), (1,)), ((), ())), preferred_element_type=f32).astype(bf16)
+
+    for n, e in ((0, 0), (1, LZ - 1)):
+        xy[n] = by_channel(x_ref[:, e].reshape(LX * LZ, C))
+        xz[n] = by_channel(xf[pl.ds(e, LX * LY, stride=LZ), :].astype(bf16))
 
     def tap_of(p):
         return p % 9 // 3, p % 3, (1, early_tap, late_tap)[p // 9]
 
-    def pair_main(q, h):
+    for p in range(0, 27, 2):
         views = []
-        for p in (4 * q + 2 * h, 4 * q + 2 * h + 1):
-            if p < 27:
-                a, b, c = tap_of(p)
-                views.append(pad[c, 2 - a : 2 - a + LX, 2 - b : 2 - b + LY].reshape(CELLS, C))
+        for t in range(p, min(p + 2, 27)):
+            a, b, c = tap_of(t)
+            views.append(pad[c, 2 - a : 2 - a + LX, 2 - b : 2 - b + LY].reshape(CELLS, C))
         v = jnp.concatenate(views, axis=1) if len(views) == 2 else views[0]
         o = jnp.dot(xt[...], v, preferred_element_type=f32)
-        return o if len(views) == 2 else jnp.concatenate([o, jnp.zeros((C, C), f32)], axis=1)
-
-    def pair_rest(q, h):
-        views = []
-        for p in (4 * q + 2 * h, 4 * q + 2 * h + 1):
-            if p < 27:
-                a, b, _ = tap_of(p)
-                views.append(turned[b, 2 - a : 2 - a + LX].reshape(LX * LY, C))
-            else:
-                views.append(jnp.zeros((LX * LY, C), bf16))
-        return jnp.dot(xz[...], jnp.concatenate(views, axis=1), preferred_element_type=f32)
-
-    def main(q):
-        for h in range(2):
-            base[2 * (q - 4) + h] = pair_main(q, h)
+        for n in range(len(views)):
+            grad[p + n] = o[:, n * C : (n + 1) * C]
+    grad[27] = jnp.zeros((C, C), f32)
+
+    def add_side(lhs, taps, view):
+        o = jnp.dot(lhs, jnp.concatenate([view(p) for p in taps], axis=1), preferred_element_type=f32)
+        for n, p in enumerate(taps):
+            grad[p] += o[:, n * C : (n + 1) * C]
 
     def quad(q):
-        outs = []
-        for h in range(2):
-            if q < 4:
-                o = pair_main(q, h)
-            else:
-                o = base[2 * (q - 4) + h]
-                if 4 * q + 2 * h >= 18:
-                    o = o + pair_rest(q, h)
-            outs += [o[:, :C], o[:, C:]]
+        outs = [grad[p] for p in range(4 * q, 4 * q + 4)]
         low = lax.broadcasted_iota(jnp.int32, (16, 8, C), 1) < 4
         pieces = [[], []]
         for h in range(2):
@@ -398,8 +402,34 @@
             ).start()
 
     by_neighbours(flat_rows, hr.at[0])
+    for e, yr in ((0, 0), (1, LY + 1)):
+        face = land_y[e]
+        pad[1, 1 : LX + 1, yr] = face
+        full[1 : LX + 1, yr, 8 : 8 + LZ, :] = face.astype(f32)
+        pad[0, 1 : LX + 1, yr] = full[1 : LX + 1, yr, 9 : 9 + LZ, :].astype(bf16)
+        pad[2, 1 : LX + 1, yr] = full[1 : LX + 1, yr, 7 : 7 + LZ, :].astype(bf16)
+
+        def view_y(p, yr=yr):
+            a, _, c = tap_of(p)
+            return pad[c, 2 - a : 2 - a + LX, yr].reshape(LX * LZ, C)
+
+        add_side(xy[e], [p for p in range(27) if p % 3 == (2 if e == 0 else 0)], view_y)
+    for k, xr in ((0, 0), (1, LX + 1)):
+        pad[1, xr, 1 : LY + 1] = land_x[k]
+        full[xr, 1 : LY + 1, 8 : 8 + LZ, :] = land_x[k].astype(f32)
+        for e, yr in ((0, 0), (1, LY + 1)):
+            pad[1, xr, yr] = land_c[k, e]
+            full[xr, yr, 8 : 8 + LZ, :] = land_c[k, e].astype(f32)
+        shift(xr, 0)
+
+        def view_x(p, xr=xr):
+            _, b, c = tap_of(p)
+            return pad[c, xr, 2 - b : 2 - b + LY].reshape(LY * LZ, C)
+
+        cells = LY * LZ
+        lhs = xt[:, :cells] if k == 0 else xt[:, CELLS - cells :]
+        add_side(lhs, [p for p in range(27) if p % 9 // 3 == (2 if k == 0 else 0)], view_x)
     quads(0)
-
     def lay_out(side):
         for i in range(10):
             plane[side, i, 8 : 8 + LY, :] = zhalo[side, i].astype(f32)
@@ -408,6 +438,10 @@
                     plane[side, i, yr : yr + 1, :] = zcorner[side, e, i - 1 : i, :]
                 else:
                     plane[side, i, yr : yr + 1, :] = zdot[side, e, i // 9]
+        for i in range(10):
+            turned[1, i] = zhalo[side, i]
+            for b in (0, 2):
+                turned[b, i] = plane[side, i, 9 - b : 9 - b + LY, :].astype(bf16)
 
     def put_in(side):
         zr = 7 + 17 * side
@@ -418,25 +452,15 @@
 
         lax.fori_loop(0, 10, put, 0)
 
+    def view_z(p):
+        a, b, _ = tap_of(p)
+        return turned[b, 2 - a : 2 - a + LX].reshape(LX * LY, C)
+
     wide_wait(False)
-
     lay_out(early_side)
-    put_in(early_side)
-    for i in (0, 9):
-        full[i, :, 8 : 8 + LZ, :] = pad[1, i].astype(f32)
-    for j in (0, 17):
-        full[1 : LX + 1, j, 8 : 8 + LZ, :] = pad[1, 1 : LX + 1, j].astype(f32)
-
-    def shift(i, _):
-        pad[0, i] = full[i, :, 9 : 9 + LZ, :].astype(bf16)
-        pad[2, i] = full[i, :, 7 : 7 + LZ, :].astype(bf16)
-        return 0
-
-    lax.fori_loop(0, 10, shift, 0)
+    add_side(xz[early_side], range(9, 18), view_z)
     quads(1)
     spread_chunk(0)
-    for q in range(4, 7):
-        main(q)
     drain(part.at[pl.ds(0, 31)], wr.at[1])
     drain(raws.at[pl.ds(0, 3)], wr.at[0])
     total = part[0]
@@ -470,10 +494,7 @@
     spread_chunk(1)
     wide_wait(True)
     lay_out(late_side)
-    for i in range(10):
-        turned[1, i] = zhalo[late_side, i]
-        for b in (0, 2):
-            turned[b, i] = plane[late_side, i, 9 - b : 9 - b + LY, :].astype(bf16)
+    add_side(xz[late_side], range(18, 27), view_z)
     quads(2)
     spread_chunk(2)
     def hand_on(h):
@@ -491,18 +512,20 @@
         def one(i, _):
             views = []
             for a, b, c in TAPS[14 * h : 14 + 13 * h]:
-                views.append(pad[c, i + 2 - a, 2 - b : 2 - b + LY].reshape(LY * LZ, C))
+                views.append(pad[c, pl.ds(2 * i + 2 - a, 2), 2 - b : 2 - b + LY].reshape(2 * LY * LZ, C))
             out = jnp.dot(jnp.concatenate(views, axis=1), wt[halves[h], :], preferred_element_type=f32)
             if h == 0:
                 part_dx[i] = out
             else:
-                dx_ref[i] = (part_dx[i] + out).astype(bf16).reshape(LY, LZ, C)
+                dx_ref[pl.ds(2 * i, 2)] = (part_dx[i] + out).astype(bf16).reshape(2, LY, LZ, C)
             return 0
 
         lax.fori_loop(lo, hi, one, 0)
 
-    put_in(late_side)
+    put_in(0)
+    put_in(1)
     lax.fori_loop(0, 10, shift, 0)
+    hand_on(0)
     drain(r1, got.at[1])
     for q in range(7):
         acc = own[q, mine] + precv[q, mine].astype(f32)
@@ -519,9 +542,8 @@
     for k in (4, 3, 5, 2, 6, 1, 7):
         remote(rows.at[spots[k][0]], r2.at[z], got.at[2], z_peer(k)).start()
 
-    hand_on(0)
     take_over(0)
-    input_grad(0, 0, 8)
+    input_grad(0, 0, 4)
     hand_on(1)
     drain(r2.at[pl.ds(0, 7)], got.at[2])
     acc = r2[0].astype(f32)
@@ -532,7 +554,7 @@
     for k in (2, 1, 3):
         remote(gath.at[x], gath.at[x], got.at[3], x_peer(k)).start()
     take_over(1)
-    input_grad(1, 0, 4)
+    input_grad(1, 0, 2)
 
     drain(gath.at[pl.ds(0, 3)], got.at[3])
     for r in range(4):
@@ -550,7 +572,7 @@
         remote(stat.at[here], stat.at[here], got.at[4], device).start()
 
     to_plane(send_stat)
-    input_grad(1, 4, 8)
+    input_grad(1, 2, 4)
     drain(stat.at[pl.ds(0, 31)], got.at[4])
     total = stat[0]
     for j in range(1, 32):
@@ -618,14 +640,18 @@
             vmem((3, 10, LY, C), bf16),
             vmem((CELLS, C), f32),
             vmem((C, CELLS), bf16),
-            vmem((C, C), bf16),
-            vmem((6, C, 2 * C), f32),
+            vmem((2, C, C), bf16),
+            vmem((2, C, C), bf16),
+            vmem((28, C, C), f32),
+            vmem((2, LY, LZ, C), bf16),
+            vmem((2, LX, LZ, C), bf16),
+            vmem((2, 2, LZ, C), bf16),
             vmem((4, 27, 4, C), f32),
             vmem((27, 16, C), f32),
             vmem((32, 2, C), f32),
             vmem((C, 27 * C), bf16),
             vmem((27 * C, C), bf16),
-            vmem((LX, LY * LZ, C), f32),
+            vmem((LX // 2, 2 * LY * LZ, C), f32),
             vmem((7, 16, 16, C), f32),
             vmem((7, 16, 16, C), bf16),
             vmem((7, 16, 16, C), bf16),

time: 42.2 us -> 41 us (0.972)
  Pallas kernels: 41.5 us -> 40.3 us
    pallas_call x1, Pallas kernels: 40.7 us -> 39.4 us  [on_device(): pl.pallas_call(body, out_shape=(pltpu.VMEM(inputs.shape, bf16), pltpu.VME...]
where the time goes in v3:
time: 41 us; the launch traced here: 40.9 us
  Pallas kernels  40.3 us (98%)
  between operations  0.64 us (2%)
    pallas_call x1, Pallas kernels, on_device(): pl.pallas_call(body, out_shape=(pltpu.VMEM(inputs.shape, bf16), pltpu.VME...  39.4 us

profile of v3, /device:TPU:1, one launch (start us, length us, event | category | flops | bytes accessed | tf_op | source)
XLA Modules:
  0.0 40.9 jit_solution(13338494540193582581)
XLA Ops:
  0.6 39.4 %shard_map.50 = (bf16[8,16,16,128]{3,2,1,0:T(8,128)(2,1)S(1)}, f32[27,4,128]{2,1,0:T(4,128)S(1)}) custom-call(f32[27,4,128]{2,1,0:T(4,128)} %bitcast.2, bf16[8,16,16,128]{3,2,1,0:T(8,128)(2,1)} %x_hbm.1, bf16[8,16,16,128]{3,2,1,0:T(8,128)(2,1)} %cot_hbm.1), custom_call_target="tpu_custom_call" | custom-call | tf_op jit(solution)/shard_map/pallas_call | solution.py:619
  40.1 0.8 %shard_map.51 = (bf16[8,16,16,128]{3,2,1,0:T(8,128)(2,1)}, f32[27,4,128]{2,1,0:T(4,128)}) custom-call(bf16[8,16,16,128]{3,2,1,0:T(8,128)(2,1)S(1)} %get-tuple-element.6.dx_in, f32[27,4,128]{2,1,0:T(4,128)S(1)} %get-tuple-element.7.dw_in), custom_call_target="tpu_custom_call" | custom-call | tf_op jit(solution)/shard_map/pallas_call | solution.py:680

commit v4 on v3

--- a/solution.py
+++ b/solution.py
@@ -34,7 +34,7 @@
 
 def body(raw_hbm, x_hbm, cot_hbm, dx_ref, dw_ref, raw_ref, x_ref, cot_ref,
          full, pad, zface, zedge, zpoint, zhalo, zcorner, zdot, plane, turned, xf, xt, xy, xz, grad, land_x, land_y, land_c,
-         raws, mine_raw, part, w, wt, part_dx, own, psend, precv, spread, r1, red, comp, r2, rows, gath, nat, mine_std, stat,
+         raws, mine_raw, part, norm, w, wt, part_dx, own, psend, precv, spread, r1, red, comp, r2, rows, gath, nat, mine_std, stat,
          ls, hr, wr, dr, ours, got, sent):
     gx, gy, gz = lax.axis_index("gx"), lax.axis_index("gy"), lax.axis_index("gz")
     def div(a, n):
@@ -49,7 +49,7 @@
     mine = gy * 4 + x
     early_tap, late_tap = 2 - 2 * z_hi, 2 * z_hi
     early_side, late_side = z_hi, 1 - z_hi
-    full2 = full.reshape(10 * 18 * PITCH, C)
+    full2 = full.reshape(11 * 18 * PITCH, C)
 
     def dev(a, b, c):
         return (a, b, c)
@@ -58,7 +58,7 @@
         zz = mod(z + step, 8)
         return mod(zz, 4), div(zz, 4)
 
-    spots = [ring(step) for step in range(8)] + [ring(2 + 4 * core)]
+    spots = [ring(step) for step in range(8)] + [ring(2 + 4 * core), (mod(z_lo + 2, 4), z_hi)]
     at_gz = [hi * 4 + x for _, hi in spots]
     at_gx = [[lo * 2 + core, lo * 2 + 1 - core] for lo, _ in spots]
     at_gy = [gy] + [mod(gy + k, 4) for k in range(1, 4)]
@@ -81,8 +81,8 @@
     def plane_peer(k, step):
         return dev(at_gx[step][k // 4], at_gy[k % 4], at_gz[step])
 
-    def to_plane(send, steps=(2, 1, 7, 0)):
-        for step in steps:
+    def to_plane(send):
+        for step in (9, 1, 7, 0):
             for k in range(1 if step == 0 else 0, 8):
                 send(plane_peer(k, step))
 
@@ -138,11 +138,11 @@
             greet(dev(gx + d[0], gy + d[1], gz + d[2]))
 
         greeted = greeted + there.astype(jnp.int32)
-    for k in (4, 3, 5, 2):
-        greet(z_peer(k))
+    greet(z_peer(2))
+    greet(z_peer(6))
     for k in (10, 11, 9, 6, 14, 5, 7, 13, 15, 1, 2, 3):
         greet(xy_peer(k))
-    to_plane(greet, (6, 1, 7, 0))
+    to_plane(greet)
 
     loads[0].wait()
 
@@ -164,9 +164,10 @@
         for e, yr in ((0, 1), (1, LY)):
             for i in range(LX):
                 at = ((i + 1) * 18 + yr) * PITCH + zr
-                zedge[s, e, i : i + 1, :] = full2[at : at + 1, :]
-            zpoint[s, e, 0] = zedge[s, e, 0:1, :]
-            zpoint[s, e, 1] = zedge[s, e, LX - 1 : LX, :]
+                plane[s, e, i : i + 1, :] = full2[at : at + 1, :]
+            zedge[s, e] = plane[s, e, 0:LX, :].astype(bf16)
+            zpoint[s, e, 0] = plane[s, e, 0:1, :]
+            zpoint[s, e, 1] = plane[s, e, LX - 1 : LX, :]
     loads[1].wait()
     raws[gy] = raw_ref[...]
     first = jnp.zeros((4, C), f32)
@@ -178,7 +179,7 @@
     part[gx * 4 + gy, 0:1, :] = jnp.sum(first, axis=0, keepdims=True)
     part[gx * 4 + gy, 1:2, :] = jnp.sum(second, axis=0, keepdims=True)
 
-    pl.semaphore_wait(barrier, greeted + (4 + 12 + 31))
+    pl.semaphore_wait(barrier, greeted + (2 + 12 + 31))
 
     def halo_copy(d):
         dx, dy, dz = d
@@ -213,9 +214,17 @@
         here = part.at[gx * 4 + gy]
         remote(here, here, wr.at[1], device).start()
 
+    busy = jnp.logical_or(gz == 3, gz == 4)
+
+    def large(d):
+        return d[1] == 0 and d[2] == 0
+
     for d in DIRECTIONS:
-
-        @pl.when(present(d))
+        there = present(d)
+        if large(d):
+            there = jnp.logical_and(there, jnp.logical_not(busy))
+
+        @pl.when(there)
         def _(d=d):
             halo_copy(d).start()
 
@@ -225,7 +234,7 @@
         return 128 * nx + 64 * ny + 8 * nx * ny
 
     def wide_rows(nx, ny):
-        return 64 + 8 * nx + 8 * ny + nx * ny
+        return 64 + 8 * nx + 4 * ny + nx * ny
 
     def by_neighbours(rows, sem):
         for nx in (1, 2):
@@ -297,7 +306,7 @@
 
             @pl.when(jnp.logical_not(both))
             def _(r=r, e=e):
-                zcorner[r, e] = jnp.zeros((8, C), f32)
+                zcorner[r, e] = jnp.zeros((8, C), bf16)
 
             for k, x_there in ((0, gx > 0), (1, gx < 7)):
 
@@ -333,6 +342,13 @@
             (((1,), (1,)), ((), ())),
             preferred_element_type=f32,
         ).astype(bf16)
+
+    for d in DIRECTIONS:
+        if large(d):
+
+            @pl.when(jnp.logical_and(present(d), busy))
+            def _(d=d):
+                halo_copy(d).start()
 
     def widen(i, _):
         xf[pl.ds(pl.multiple_of(i * LY * LZ, LY * LZ), LY * LZ), :] = x_ref[i].reshape(LY * LZ, C).astype(f32)
@@ -431,11 +447,12 @@
         add_side(lhs, [p for p in range(27) if p % 9 // 3 == (2 if k == 0 else 0)], view_x)
     quads(0)
     def lay_out(side):
+        edges = [zcorner[side, e].astype(f32) for e in range(2)]
         for i in range(10):
             plane[side, i, 8 : 8 + LY, :] = zhalo[side, i].astype(f32)
             for e, yr in ((0, 7), (1, 8 + LY)):
                 if 0 < i < 9:
-                    plane[side, i, yr : yr + 1, :] = zcorner[side, e, i - 1 : i, :]
+                    plane[side, i, yr : yr + 1, :] = edges[e][i - 1 : i]
                 else:
                     plane[side, i, yr : yr + 1, :] = zdot[side, e, i // 9]
         for i in range(10):
@@ -460,43 +477,67 @@
     lay_out(early_side)
     add_side(xz[early_side], range(9, 18), view_z)
     quads(1)
-    spread_chunk(0)
-    drain(part.at[pl.ds(0, 31)], wr.at[1])
-    drain(raws.at[pl.ds(0, 3)], wr.at[0])
-    total = part[0]
-    for j in range(1, 32):
-        total = total + part[j]
-    mean = total[0:1] / FAN
-    var = total[1:2] / FAN - mean * mean
-    inv = lax.rsqrt(var + var_eps)
-    for t in range(27):
-        for j in range(4):
-            mine_raw[t, 4 * j : 4 * j + 4, :] = raws[j, t]
-    mine_rows = pl.ds(pl.multiple_of(gx * 16, 16), 16)
-    for p in range(27):
-        a, b, c = TAPS[p]
-        t = 9 * a + 3 * b + c
-        w[mine_rows, p * C : (p + 1) * C] = ((mine_raw[t] - mean) * inv).astype(bf16)
-    for t in range(27):
-        mine_std[4 * t : 4 * t + 4, :] = (raw_ref[t] - mean) * inv
+    far = jnp.logical_or(gz == 3, gz == 4)
 
     halves = (slice(0, 14 * C), slice(14 * C, 27 * C))
 
     def slab(g, h):
         return w.at[pl.ds(pl.multiple_of(g * 16, 16), 16), halves[h]]
 
-    for h in range(2):
-        for step in (8, 1, 7):
-            remote(slab(gx, h), slab(gx, h), wr.at[2 + h], chip_peer(step)).start()
-    for h in range(2):
-        remote(slab(gx, h), slab(gx, h), ours.at[h], partner).start()
-
+    def filter_rows():
+        drain(part.at[pl.ds(0, 31)], wr.at[1])
+        drain(raws.at[pl.ds(0, 3)], wr.at[0])
+        total = part[0]
+        for j in range(1, 32):
+            total = total + part[j]
+        mean = total[0:1] / FAN
+        var = total[1:2] / FAN - mean * mean
+        inv = lax.rsqrt(var + var_eps)
+        norm[0:1, :] = mean
+        norm[1:2, :] = var
+        norm[2:3, :] = inv
+        for t in range(27):
+            for j in range(4):
+                mine_raw[t, 4 * j : 4 * j + 4, :] = raws[j, t]
+        mine_rows = pl.ds(pl.multiple_of(gx * 16, 16), 16)
+        for p in range(27):
+            a, b, c = TAPS[p]
+            t = 9 * a + 3 * b + c
+            w[mine_rows, p * C : (p + 1) * C] = ((mine_raw[t] - mean) * inv).astype(bf16)
+        for t in range(27):
+            mine_std[4 * t : 4 * t + 4, :] = (raw_ref[t] - mean) * inv
+        for h in range(2):
+            for step in (8, 1, 7):
+                remote(slab(gx, h), slab(gx, h), wr.at[2 + h], chip_peer(step)).start()
+        for h in range(2):
+            remote(slab(gx, h), slab(gx, h), ours.at[h], partner).start()
+
+    def finish():
+        wide_wait(True)
+        lay_out(late_side)
+        add_side(xz[late_side], range(18, 27), view_z)
+        quads(2)
+
+    @pl.when(jnp.logical_not(far))
+    def _():
+        finish()
+
+    spread_chunk(0)
     spread_chunk(1)
-    wide_wait(True)
-    lay_out(late_side)
-    add_side(xz[late_side], range(18, 27), view_z)
-    quads(2)
+
+    @pl.when(far)
+    def _():
+        filter_rows()
+        finish()
+
     spread_chunk(2)
+
+    @pl.when(jnp.logical_not(far))
+    def _():
+        filter_rows()
+
+    mean, var, inv = norm[0:1, :], norm[1:2, :], norm[2:3, :]
+
     def hand_on(h):
         drain(w.at[pl.ds(0, 48), halves[h]], wr.at[2 + h])
         for k in (1, 2, 3):
@@ -628,17 +669,17 @@
             vmem((27, 4, C), f32),
             vmem((LX, LY, LZ, C), bf16),
             vmem((LX, LY, LZ, C), bf16),
-            vmem((10, 18, PITCH, C), f32),
+            vmem((11, 18, PITCH, C), f32),
             vmem((3, 10, 18, LZ, C), bf16),
             vmem((2, LX, LY, C), bf16),
-            vmem((2, 2, 8, C), f32),
+            vmem((2, 2, 8, C), bf16),
             vmem((2, 2, 2, 1, C), f32),
             vmem((2, 10, LY, C), bf16),
-            vmem((2, 2, 8, C), f32),
+            vmem((2, 2, 8, C), bf16),
             vmem((2, 2, 2, 1, C), f32),
             vmem((2, 10, 32, C), f32),
             vmem((3, 10, LY, C), bf16),
-            vmem((CELLS, C), f32),
+            vmem((CELLS + LZ, C), f32),
             vmem((C, CELLS), bf16),
             vmem((2, C, C), bf16),
             vmem((2, C, C), bf16),
@@ -649,6 +690,7 @@
             vmem((4, 27, 4, C), f32),
             vmem((27, 16, C), f32),
             vmem((32, 2, C), f32),
+            vmem((8, C), f32),
             vmem((C, 27 * C), bf16),
             vmem((27 * C, C), bf16),
             vmem((LX // 2, 2 * LY * LZ, C), f32),
@@ -662,7 +704,7 @@
             vmem((8, 32, C), bf16),
             vmem((4, 32, C), bf16),
             vmem((4, 32, C), f32),
-            vmem((112, C), f32),
+            vmem((120, C), f32),
             vmem((112, C), f32),
             vmem((32, 4, C), f32),
             dma((3,)),

time: 41 us -> 40.2 us (0.980)
  Pallas kernels: 40.3 us -> 39.5 us
    pallas_call x1, Pallas kernels: 39.4 us -> 38.7 us  [on_device(): pl.pallas_call(body, out_shape=(pltpu.VMEM(inputs.shape, bf16), pltpu.VME...]
where the time goes in v4:
time: 40.2 us; the launch traced here: 40.1 us
  Pallas kernels  39.5 us (98%)
  between operations  0.64 us (2%)
    pallas_call x1, Pallas kernels, on_device(): pl.pallas_call(body, out_shape=(pltpu.VMEM(inputs.shape, bf16), pltpu.VME...  38.7 us
    pallas_call x1, Pallas kernels, on_device(): pl.pallas_call(hand_over, out_shape=(jax.ShapeDtypeStruct(dx.shape, bf16)...  0.81 us

profile of v4, /device:TPU:1, one launch (start us, length us, event | category | flops | bytes accessed | tf_op | source)
XLA Modules:
  0.0 40.1 jit_solution(16365308765904062692)
XLA Ops:
  0.6 38.7 %shard_map.50 = (bf16[8,16,16,128]{3,2,1,0:T(8,128)(2,1)S(1)}, f32[27,4,128]{2,1,0:T(4,128)S(1)}) custom-call(f32[27,4,128]{2,1,0:T(4,128)} %bitcast.2, bf16[8,16,16,128]{3,2,1,0:T(8,128)(2,1)} %x_hbm.1, bf16[8,16,16,128]{3,2,1,0:T(8,128)(2,1)} %cot_hbm.1), custom_call_target="tpu_custom_call" | custom-call | tf_op jit(solution)/shard_map/pallas_call | solution.py:660
  39.3 0.8 %shard_map.51 = (bf16[8,16,16,128]{3,2,1,0:T(8,128)(2,1)}, f32[27,4,128]{2,1,0:T(4,128)}) custom-call(bf16[8,16,16,128]{3,2,1,0:T(8,128)(2,1)S(1)} %get-tuple-element.6.dx_in, f32[27,4,128]{2,1,0:T(4,128)S(1)} %get-tuple-element.7.dw_in), custom_call_target="tpu_custom_call" | custom-call | tf_op jit(solution)/shard_map/pallas_call | solution.py:722

commit v5 on v4

--- a/solution.py
+++ b/solution.py
@@ -256,7 +256,6 @@
 
     for k in (2, 1, 3):
         remote(raw_ref, raws.at[gy], wr.at[0], gy_peer(k)).start()
-    to_plane(send_part)
 
     tile = jnp.zeros((LZ, C), bf16)
 
@@ -350,6 +349,8 @@
             def _(d=d):
                 halo_copy(d).start()
 
+    to_plane(send_part)
+
     def widen(i, _):
         xf[pl.ds(pl.multiple_of(i * LY * LZ, LY * LZ), LY * LZ), :] = x_ref[i].reshape(LY * LZ, C).astype(f32)
         return 0
@@ -381,8 +382,12 @@
         for n, p in enumerate(taps):
             grad[p] += o[:, n * C : (n + 1) * C]
 
-    def quad(q):
+    def quad(q, late=None):
         outs = [grad[p] for p in range(4 * q, 4 * q + 4)]
+        if late is not None:
+            for n, p in enumerate(range(4 * q, 4 * q + 4)):
+                if 18 <= p < 27:
+                    outs[n] = outs[n] + late[:, (p - 18) * C : (p - 17) * C]
         low = lax.broadcasted_iota(jnp.int32, (16, 8, C), 1) < 4
         pieces = [[], []]
         for h in range(2):
@@ -396,10 +401,10 @@
                 own[q, 2 * j + e] = t[j]
                 psend[q, 2 * j + e] = t[8 + j].astype(bf16)
 
-    def quads(n):
+    def quads(n, late=None):
         lo, hi = CHUNKS[n]
         for q in range(lo, hi):
-            quad(q)
+            quad(q, late)
         some = pl.ds(lo, hi - lo)
         remote(psend.at[some], precv.at[some], dr.at[n], partner).start()
 
@@ -515,8 +520,8 @@
     def finish():
         wide_wait(True)
         lay_out(late_side)
-        add_side(xz[late_side], range(18, 27), view_z)
-        quads(2)
+        late = jnp.concatenate([view_z(p) for p in range(18, 27)], axis=1)
+        quads(2, jnp.dot(xz[late_side], late, preferred_element_type=f32))
 
     @pl.when(jnp.logical_not(far))
     def _():

time: 40.2 us -> 40 us (level)
  no operation moved by 1% of the time
where the time goes in v5:
time: 40 us; the launch traced here: 39.9 us
  Pallas kernels  39.3 us (98%)
  between operations  0.64 us (2%)
    pallas_call x1, Pallas kernels, on_device(): pl.pallas_call(body, out_shape=(pltpu.VMEM(inputs.shape, bf16), pltpu.VME...  38.5 us
    pallas_call x1, Pallas kernels, on_device(): pl.pallas_call(hand_over, out_shape=(jax.ShapeDtypeStruct(dx.shape, bf16)...  0.81 us

profile of v5, /device:TPU:1, one launch (start us, length us, event | category | flops | bytes accessed | tf_op | source)
XLA Modules:
  0.0 39.9 jit_solution(6581081785178765867)
XLA Ops:
  0.6 38.5 %shard_map.50 = (bf16[8,16,16,128]{3,2,1,0:T(8,128)(2,1)S(1)}, f32[27,4,128]{2,1,0:T(4,128)S(1)}) custom-call(f32[27,4,128]{2,1,0:T(4,128)} %bitcast.2, bf16[8,16,16,128]{3,2,1,0:T(8,128)(2,1)} %x_hbm.1, bf16[8,16,16,128]{3,2,1,0:T(8,128)(2,1)} %cot_hbm.1), custom_call_target="tpu_custom_call" | custom-call | tf_op jit(solution)/shard_map/pallas_call | solution.py:665
  39.1 0.8 %shard_map.51 = (bf16[8,16,16,128]{3,2,1,0:T(8,128)(2,1)}, f32[27,4,128]{2,1,0:T(4,128)}) custom-call(bf16[8,16,16,128]{3,2,1,0:T(8,128)(2,1)S(1)} %get-tuple-element.6.dx_in, f32[27,4,128]{2,1,0:T(4,128)S(1)} %get-tuple-element.7.dw_in), custom_call_target="tpu_custom_call" | custom-call | tf_op jit(solution)/shard_map/pallas_call | solution.py:727

commit v6 on v5

--- a/solution.py
+++ b/solution.py
@@ -403,15 +403,20 @@
 
     def quads(n, late=None):
         lo, hi = CHUNKS[n]
+        step = 1 if n == 2 else hi - lo
         for q in range(lo, hi):
             quad(q, late)
-        some = pl.ds(lo, hi - lo)
-        remote(psend.at[some], precv.at[some], dr.at[n], partner).start()
+            if (q - lo) % step == step - 1:
+                some = pl.ds(q - step + 1, step)
+                remote(psend.at[some], precv.at[some], dr.at[q - 2 if n == 2 else n], partner).start()
 
     def spread_chunk(n):
         lo, hi = CHUNKS[n]
-        drain(precv.at[pl.ds(lo, hi - lo)], dr.at[n])
+        if n < 2:
+            drain(precv.at[pl.ds(lo, hi - lo)], dr.at[n])
         for q in range(lo, hi):
+            if n == 2:
+                drain(precv.at[pl.ds(q, 1)], dr.at[q - 2])
             spread[:, q] = (own[q] + precv[q].astype(f32)).astype(bf16)
 
         for k in (10, 11, 9, 6, 14, 2, 8, 5, 7, 13, 15, 1, 3, 4, 12):
@@ -715,7 +720,7 @@
             dma((3,)),
             dma((3,)),
             dma((4,)),
-            dma((3,)),
+            dma((5,)),
             dma((2,)),
             dma((5,)),
             dma((1,)),

time: 40 us -> 40.2 us (level)
  no operation moved by 1% of the time
where the time goes in v6:
time: 40.2 us; the launch traced here: 40.1 us
  Pallas kernels  39.4 us (98%)
  between operations  0.64 us (2%)
    pallas_call x1, Pallas kernels, on_device(): pl.pallas_call(body, out_shape=(pltpu.VMEM(inputs.shape, bf16), pltpu.VME...  38.6 us
    pallas_call x1, Pallas kernels, on_device(): pl.pallas_call(hand_over, out_shape=(jax.ShapeDtypeStruct(dx.shape, bf16)...  0.81 us

profile of v6, /device:TPU:1, one launch (start us, length us, event | category | flops | bytes accessed | tf_op | source)
XLA Modules:
  0.0 40.1 jit_solution(14556950933796893744)
XLA Ops:
  0.6 38.6 %shard_map.50 = (bf16[8,16,16,128]{3,2,1,0:T(8,128)(2,1)S(1)}, f32[27,4,128]{2,1,0:T(4,128)S(1)}) custom-call(f32[27,4,128]{2,1,0:T(4,128)} %bitcast.2, bf16[8,16,16,128]{3,2,1,0:T(8,128)(2,1)} %x_hbm.1, bf16[8,16,16,128]{3,2,1,0:T(8,128)(2,1)} %cot_hbm.1), custom_call_target="tpu_custom_call" | custom-call | tf_op jit(solution)/shard_map/pallas_call | solution.py:670
  39.2 0.8 %shard_map.51 = (bf16[8,16,16,128]{3,2,1,0:T(8,128)(2,1)}, f32[27,4,128]{2,1,0:T(4,128)}) custom-call(bf16[8,16,16,128]{3,2,1,0:T(8,128)(2,1)S(1)} %get-tuple-element.6.dx_in, f32[27,4,128]{2,1,0:T(4,128)S(1)} %get-tuple-element.7.dw_in), custom_call_target="tpu_custom_call" | custom-call | tf_op jit(solution)/shard_map/pallas_call | solution.py:732
